TPU v7x, 32 devices: a whole 2x2x4 slice. The times are simulated.
32 devices in a mesh: replica: 8 (over z, x), shard: 4 (over y, core).
Axes of the slice: x: 2, y: 2, z: 4, core: 2. Of those that a mesh axis runs over, the one named last changes fastest.
Arguments:
- deltas: bfloat16 [8, 2048, 8192], P('replica', 'shard')
- master: float32 [2048, 8192], P('shard', 'replica'), may hold values from -6 to 6
- momentum: float32 [2048, 8192], P('shard', 'replica'), may hold values from -6 to 6
- block_owner: int32 [8, 1], replicated, may hold values from 0 to 3; in each aligned block of 8 rows (0 to 7, 8 to 15, ...) at most 4 rows name the same one
Outputs:
- master_out: float32 [2048, 8192], P('shard', 'replica')
- momentum_out: float32 [2048, 8192], P('shard', 'replica')
- params: bfloat16 [1024, 8192], P(None, 'replica')
Inputs may be any that keep to these rules, and one draw needn't show every extreme that they name: `block_owner`: every shard owns at least one block and at most 4; some shard owns exactly 4. Rows of slots that are not live hold arbitrary deltas.
All inputs are finite; a program needn't handle non-finite values.
Results may differ from a plain program's by a relative error of at most 0.01.
Values may be sent and summed in bfloat16 or wider, within the bound.
A program may use at most 128 MiB of HBM per device.

v0:
```python
import functools

import jax
import jax.numpy as jnp
from jax import lax
from jax.experimental import pallas as pl
from jax.experimental.pallas import tpu as pltpu
from jax.sharding import PartitionSpec as P

BLOCK_ROWS = 128
SLOTS = 4
F32 = jnp.float32
BF16 = jnp.bfloat16
VMEM_LIMIT = 56 * 1024 * 1024


def remote(src, dst, send, recv, device):
    return pltpu.make_async_remote_copy(
        src_ref=src, dst_ref=dst, send_sem=send, recv_sem=recv,
        device_id=device, device_id_type=pl.DeviceIdType.MESH,
    )


def shard_count(owner, shard):
    return sum(jnp.where(owner[b, 0] == shard, 1, 0) for b in range(owner.shape[0]))


def spread(condition, shape):
    return jnp.broadcast_to(jnp.where(condition, 1, 0), shape) != 0


def sync_kernel(
    R, S, rows, rc,
    owner, deltas, master, momentum,
    sums, bases, tot,
    dv, p3, yt, ms, mm, base, xin, pair, zin, mine, norm, nbuf, sbuf,
    ld, lm, p3_s, p3_r, t_s, t_r, x_s, x_r, z_s, z_r, l_s, c_s, c_r, y_s, y_r, f_s, f_r,
    bl_s, bc_s, bc_r, by_s, by_r, bf_s, bf_r, n_s, n_r, m_s, m_r,
):
    width = deltas.shape[2]
    cols = width // R
    Z, O = R // 2, S // 2
    per = BLOCK_ROWS // rc
    half = BLOCK_ROWS // 2
    chunks = rows // rc
    quad = rows < SLOTS * BLOCK_ROWS
    whole = rows // BLOCK_ROWS
    direct = whole * per
    top = whole * BLOCK_ROWS
    me_r, me_s = lax.axis_index("replica"), lax.axis_index("shard")
    z, x = me_r // 2, me_r % 2
    o, core = me_s // 2, me_s % 2
    x_peer = z * 2 + 1 - x
    twin = o * 2 + 1 - core

    barrier = pltpu.get_barrier_semaphore()
    for i in range(1, R):
        pl.semaphore_signal(barrier, inc=1, device_id=((me_r + i) % R, me_s), device_id_type=pl.DeviceIdType.MESH)
    for i in range(1, S):
        pl.semaphore_signal(barrier, inc=1, device_id=(me_r, (me_s + i) % S), device_id_type=pl.DeviceIdType.MESH)

    def load(k):
        part = pl.ds(k * BLOCK_ROWS, BLOCK_ROWS)
        return pltpu.make_async_copy(deltas.at[0, part, :], dv.at[part, :], ld.at[k])

    if quad:
        load(whole).start()
    for k in range(whole):
        load(k).start()
    load_master = pltpu.make_async_copy(master, ms, lm.at[0])
    load_momentum = pltpu.make_async_copy(momentum, mm, lm.at[1])
    load_master.start()
    load_momentum.start()
    mine_count = jnp.sum(jnp.where(owner[...] == me_s, 1, 0), axis=0, keepdims=True)
    twin_count = jnp.sum(jnp.where(owner[...] == twin, 1, 0), axis=0, keepdims=True)
    heavy = jnp.maximum(mine_count, twin_count) >= SLOTS
    pl.semaphore_wait(barrier, R + S - 2)

    def rows_of(c):
        return pl.ds(pl.multiple_of(c * rc, rc), rc)

    def columns(c, j, side):
        return pl.ds(pl.multiple_of((((z + 1 + j) % Z) * 2 + side) * cols, cols), cols)

    def x_copy(source, c, j):
        return remote(
            source.at[rows_of(c), columns(c, j, 1 - x)], xin.at[c, j], x_s.at[c, j], x_r.at[c, j], (x_peer, me_s)
        )

    def z_copy(c, j):
        return remote(
            pair.at[c, j], zin.at[c, j], z_s.at[c, j], z_r.at[c, j], (((z + 1 + j) % Z) * 2 + x, me_s)
        )

    def c_copy(c):
        return remote(mine.at[c], sums.at[me_s, c], c_s.at[c], c_r.at[c], (me_r, twin))

    def l_copy(c):
        return pltpu.make_async_copy(mine.at[c], sums.at[me_s, c], l_s.at[c])

    def y_copy(i, c):
        return remote(
            mine.at[c], sums.at[me_s, c], y_s.at[i - 1, c], y_r.at[i - 1, c], (me_r, ((o + i) % O) * 2 + core)
        )

    def f_copy(i, c):
        source = ((o + O - i) % O) * 2 + core
        return remote(sums.at[source, c], sums.at[source, c], f_s.at[i - 1, c], f_r.at[i - 1, c], (me_r, twin))

    def by_copy(i):
        return remote(base, bases.at[me_s], by_s.at[i - 1], by_r.at[i - 1], (me_r, ((o + i) % O) * 2 + core))

    def bf_copy(i):
        source = ((o + O - i) % O) * 2 + core
        return remote(bases.at[source], bases.at[source], bf_s.at[i - 1], bf_r.at[i - 1], (me_r, twin))

    def third_copy(h):
        return remote(
            deltas.at[0, pl.ds((SLOTS - 1) * BLOCK_ROWS + h * half, half), :],
            p3.at[pl.ds(h * half, half), :], p3_s.at[h], p3_r.at[h], (me_r, twin),
        )

    def t_copy():
        return remote(dv.at[pl.ds(top + half, half), :], yt, t_s, t_r, (me_r, ((o + 1) % O) * 2 + core))

    def base_twin():
        return remote(base, bases.at[me_s], bc_s, bc_r, (me_r, twin))

    def base_local():
        return pltpu.make_async_copy(base, bases.at[me_s], bl_s)

    def start_x(source, low, high):
        @pl.loop(low, high)
        def _(c):
            for j in range(Z):
                x_copy(source, c, j).start()

    def pick(condition, other, start, other_start):
        @pl.loop(0, half // 16)
        def _(r):
            keep = spread(condition, (16, 1024))
            for q in range(width // 1024):
                at = (pl.ds(pl.multiple_of(start + r * 16, 16), 16), pl.ds(q * 1024, 1024))
                there = (pl.ds(pl.multiple_of(other_start + r * 16, 16), 16), pl.ds(q * 1024, 1024))
                dv[at] = jnp.where(keep, dv[at].astype(F32), other[there].astype(F32)).astype(BF16)

    if quad:
        third_copy(1).start()
        third_copy(0).start()
    start_x(deltas.at[0], 0, direct)
    norm[0] = jnp.zeros((8, 128), F32)

    def send_third():
        load(whole).wait()
        third_copy(1).wait_recv()
        pick(mine_count >= SLOTS, p3, top + half, half)
        t_copy().start()

    def make_base():
        load_master.wait()
        load_momentum.wait()

        @pl.loop(0, SLOTS * BLOCK_ROWS // 16)
        def _(r):
            at = pl.ds(pl.multiple_of(r * 16, 16), 16)
            base[at, :] = (ms[at, :] - 0.567 * mm[at, :]).astype(BF16)

        for i in range(1, O):
            by_copy(i).start()
        base_twin().start()
        base_local().start()

    def add_pair(c):
        @pl.when(c % per == 0)
        def _():
            @pl.when(c < direct)
            def _():
                load(c // per).wait()

        for j in range(Z):
            x_copy(deltas.at[0], c, j).wait_recv()
            pair[c, j] = (xin[c, j].astype(F32) + dv[rows_of(c), columns(c, j, x)].astype(F32)).astype(BF16)
            if j < Z - 1:
                z_copy(c, j).start()

    def add_line(c):
        for j in range(Z - 1):
            z_copy(c, j).wait_recv()
        place = jnp.where(c >= direct, -1, c // per) if quad else c // per
        live = spread(place < mine_count, (8, 128))
        part = jnp.zeros((8, 128), F32)
        for r in range(0, rc, 16):
            total = pair[c, Z - 1, r:r + 16, :].astype(F32)
            for j in range(Z - 1):
                total = total + zin[c, j, r:r + 16, :].astype(F32)
            total = total / R
            mine[c, r:r + 16, :] = total.astype(BF16)
            for h in range(0, 16, 8):
                for q in range(0, cols, 128):
                    v = total[h:h + 8, q:q + 128]
                    part = part + v * v
        norm[0] = norm[0] + jnp.where(live, part, 0.0)
        for i in range(1, O):
            y_copy(i, c).start()
        c_copy(c).start()
        l_copy(c).start()

    def forward(c):
        for i in range(1, O):
            y_copy(i, c).wait_recv()
            f_copy(i, c).start()

    lag = 4

    @pl.loop(0, chunks + lag)
    def _(t):
        @pl.when(t < chunks)
        def _():
            add_pair(t)

        @pl.when(t >= lag)
        def _():
            add_line(t - lag)

        @pl.when(t == 2)
        def _():
            make_base()

        if quad:
            @pl.when(t == 0)
            def _():
                send_third()

            @pl.when(t == direct - direct // 4)
            def _():
                third_copy(0).wait_recv()
                pick(mine_count >= SLOTS, p3, top, 0)
                t_copy().wait_recv()
                pick(heavy, yt, top, 0)
                start_x(dv, direct, chunks)

    def n_copy(i):
        return remote(norm.at[0], nbuf.at[i - 1], n_s.at[i - 1], n_r.at[i - 1], ((me_r + i) % R, me_s))

    def m_copy(i):
        return remote(norm.at[1], sbuf.at[i - 1], m_s.at[i - 1], m_r.at[i - 1], (me_r, (me_s + i) % S))

    for i in range(1, R):
        n_copy(i).start()
    for i in range(1, O):
        by_copy(i).wait_recv()
        bf_copy(i).start()

    @pl.loop(0, chunks - 2)
    def _(c):
        forward(c)
        for j in range(Z):
            x_copy(deltas.at[0], c, j).wait_send()
        for j in range(Z - 1):
            z_copy(c, j).wait_send()

    total = norm[0]
    for i in range(1, R):
        n_copy(i).wait_recv()
        total = total + nbuf[i - 1]
    norm[1] = total
    for i in range(1, S):
        m_copy(i).start()

    @pl.loop(chunks - 2, chunks)
    def _(c):
        forward(c)

    for i in range(1, S):
        m_copy(i).wait_recv()
        total = total + sbuf[i - 1]
    tot[...] = total

    if quad:
        third_copy(0).wait_send()
        third_copy(1).wait_send()
        t_copy().wait_send()
    base_local().wait()
    base_twin().wait()
    for i in range(1, O):
        by_copy(i).wait_send()
        bf_copy(i).wait()
    for i in range(1, R):
        n_copy(i).wait_send()
    for i in range(1, S):
        m_copy(i).wait_send()

    @pl.loop(chunks - 2, chunks)
    def _(c):
        for j in range(Z):
            x_copy(deltas.at[0], c, j).wait_send()
        for j in range(Z - 1):
            z_copy(c, j).wait_send()

    @pl.loop(0, chunks)
    def _(c):
        l_copy(c).wait()
        c_copy(c).wait()
        for i in range(1, O):
            y_copy(i, c).wait_send()
            f_copy(i, c).wait()


def finish_kernel(
    R, units,
    owner_in, tot, master, momentum, sums, bases,
    master_out, momentum_out, params,
    owner, owner_s, ms, mm, su, pb, ps,
    a_s, b_s, u_s, p_s, q_s, oa_s, ob_s, op_s,
):
    blocks = owner.shape[0]
    cols = master.shape[1]
    half = BLOCK_ROWS // 2
    me_s = lax.axis_index("shard")
    get_owner = pltpu.make_async_copy(owner_in, owner, owner_s)
    get_owner.start()

    def unit(shard, place, h):
        if units == 2 * SLOTS:
            return shard * units + 2 * place + h
        moved = shard + jnp.where(place == SLOTS - 1, 1 - 2 * (shard % 2), 0)
        if h:
            moved = moved + jnp.where(moved // 2 == 0, 2, -2)
        return jnp.where(place < 2, shard * units + 2 * place + h, moved * units + units - 1)

    def slot_rows(j):
        return pl.ds(pl.multiple_of(j * BLOCK_ROWS, BLOCK_ROWS), BLOCK_ROWS)

    def get_slot(j):
        return [
            pltpu.make_async_copy(master.at[slot_rows(j)], ms.at[slot_rows(j)], a_s.at[j]),
            pltpu.make_async_copy(momentum.at[slot_rows(j)], mm.at[slot_rows(j)], b_s.at[j]),
        ] + [
            pltpu.make_async_copy(sums.at[unit(me_s, j, h)], su.at[2 * j + h], u_s.at[2 * j + h]) for h in range(2)
        ]

    def put_slot(j):
        return [
            pltpu.make_async_copy(ms.at[slot_rows(j)], master_out.at[slot_rows(j)], oa_s.at[j]),
            pltpu.make_async_copy(mm.at[slot_rows(j)], momentum_out.at[slot_rows(j)], ob_s.at[j]),
        ]

    def get_block(b):
        shard = owner[b, 0]
        place = sum(jnp.where(jnp.logical_and(owner[k, 0] == shard, k < b), 1, 0) for k in range(blocks))
        return [pltpu.make_async_copy(bases.at[shard * SLOTS + place], pb.at[b], p_s.at[b])] + [
            pltpu.make_async_copy(sums.at[unit(shard, place, h)], ps.at[2 * b + h], q_s.at[2 * b + h])
            for h in range(2)
        ]

    def put_block(b):
        return pltpu.make_async_copy(pb.at[b], params.at[slot_rows(b)], op_s.at[b])

    @pl.loop(0, SLOTS)
    def _(j):
        for copy in get_slot(j):
            copy.start()

    get_owner.wait()
    count = shard_count(owner, me_s)

    @pl.loop(0, blocks)
    def _(b):
        for copy in get_block(b):
            copy.start()

    total = jnp.sum(jnp.sum(tot[...], axis=1, keepdims=True), axis=0, keepdims=True)
    limit = 0.5 * jnp.sqrt(jnp.full((1, 1), blocks * BLOCK_ROWS * R * cols, F32))
    factor = jnp.minimum(1.0, limit / (jnp.sqrt(total) + 1e-06))

    @pl.loop(0, SLOTS)
    def _(j):
        for copy in get_slot(j):
            copy.wait()

        @pl.when(j < count)
        def _():
            for h in range(2):
                @pl.loop(0, half // 16)
                def _(r):
                    at = pl.ds(pl.multiple_of(j * BLOCK_ROWS + h * half + r * 16, 16), 16)
                    grad = factor * su[2 * j + h, pl.ds(pl.multiple_of(r * 16, 16), 16), :].astype(F32)
                    fresh = 0.9 * mm[at, :] + grad
                    mm[at, :] = fresh
                    ms[at, :] = ms[at, :] - 0.7 * (grad + 0.9 * fresh)

        for copy in put_slot(j):
            copy.start()

    @pl.loop(0, blocks)
    def _(b):
        for copy in get_block(b):
            copy.wait()
        for h in range(2):
            @pl.loop(0, half // 16)
            def _(r):
                at = pl.ds(pl.multiple_of(h * half + r * 16, 16), 16)
                grad = factor * ps[2 * b + h, pl.ds(pl.multiple_of(r * 16, 16), 16), :].astype(F32)
                pb[b, at, :] = (pb[b, at, :].astype(F32) - 1.33 * grad).astype(BF16)

        put_block(b).start()

    @pl.loop(0, SLOTS)
    def _(j):
        for copy in put_slot(j):
            copy.wait()

    @pl.loop(0, blocks)
    def _(b):
        put_block(b).wait()


def on_device(deltas, master, momentum, block_owner):
    R, S = lax.axis_size("replica"), lax.axis_size("shard")
    width, cols = deltas.shape[2], master.shape[1]
    blocks = block_owner.shape[0]
    half = BLOCK_ROWS // 2
    quad = S == 4 and blocks - SLOTS - (S - 2) <= 2
    rows = 2 * BLOCK_ROWS + half if quad else SLOTS * BLOCK_ROWS
    rc = half
    while rc > 16 and (rows // (rc // 2)) * R <= 160:
        rc //= 2
    chunks = rows // rc
    units = rows // half
    Z, O = R // 2, S // 2
    loads = rows // BLOCK_ROWS + (1 if quad else 0)

    dma = pltpu.SemaphoreType.DMA
    vmem = pltpu.VMEM
    anywhere = pl.BlockSpec(memory_space=pl.ANY)
    in_vmem = pl.BlockSpec(memory_space=pltpu.VMEM)
    in_smem = pl.BlockSpec(memory_space=pltpu.SMEM)
    ys, zs = max(O - 1, 1), max(Z - 1, 1)
    sums, bases, tot = pl.pallas_call(
        functools.partial(sync_kernel, R, S, rows, rc),
        out_shape=(
            jax.ShapeDtypeStruct((S, chunks, rc, cols), BF16),
            jax.ShapeDtypeStruct((S,) + master.shape, BF16),
            jax.ShapeDtypeStruct((8, 128), F32),
        ),
        in_specs=[in_vmem, anywhere, anywhere, anywhere],
        out_specs=(anywhere, anywhere, in_vmem),
        scratch_shapes=[
            vmem((loads * BLOCK_ROWS, width), BF16),
            vmem((BLOCK_ROWS, width) if quad else (16, 128), BF16),
            vmem((half, width) if quad else (16, 128), BF16),
            vmem(master.shape, F32),
            vmem(master.shape, F32),
            vmem(master.shape, BF16),
            vmem((chunks, Z, rc, cols), BF16),
            vmem((chunks, Z, rc, cols), BF16),
            vmem((chunks, zs, rc, cols), BF16),
            vmem((chunks, rc, cols), BF16),
            vmem((2, 8, 128), F32),
            vmem((R - 1, 8, 128), F32),
            vmem((S - 1, 8, 128), F32),
            dma((loads,)), dma((2,)), dma((2,)), dma((2,)), dma, dma,
            dma((chunks, Z)), dma((chunks, Z)),
            dma((chunks, zs)), dma((chunks, zs)),
            dma((chunks,)), dma((chunks,)), dma((chunks,)),
            dma((ys, chunks)), dma((ys, chunks)), dma((ys, chunks)), dma((ys, chunks)),
            dma, dma, dma,
            dma((ys,)), dma((ys,)), dma((ys,)), dma((ys,)),
            dma((R - 1,)), dma((R - 1,)), dma((S - 1,)), dma((S - 1,)),
        ],
        compiler_params=pltpu.CompilerParams(
            collective_id=0, has_side_effects=True, vmem_limit_bytes=VMEM_LIMIT
        ),
        name="sync",
    )(block_owner, deltas, master, momentum)

    return tuple(pl.pallas_call(
        functools.partial(finish_kernel, R, units),
        out_shape=(
            jax.ShapeDtypeStruct(master.shape, F32),
            jax.ShapeDtypeStruct(master.shape, F32),
            jax.ShapeDtypeStruct((blocks * BLOCK_ROWS, cols), BF16),
        ),
        in_specs=[in_vmem, in_vmem] + [anywhere] * 4,
        out_specs=(anywhere,) * 3,
        scratch_shapes=[
            pltpu.SMEM((blocks, 1), jnp.int32), dma,
            vmem(master.shape, F32),
            vmem(master.shape, F32),
            vmem((2 * SLOTS, half, cols), BF16),
            vmem((blocks, BLOCK_ROWS, cols), BF16),
            vmem((2 * blocks, half, cols), BF16),
            dma((SLOTS,)), dma((SLOTS,)), dma((2 * SLOTS,)), dma((blocks,)), dma((2 * blocks,)),
            dma((SLOTS,)), dma((SLOTS,)), dma((blocks,)),
        ],
        compiler_params=pltpu.CompilerParams(vmem_limit_bytes=VMEM_LIMIT),
        name="finish",
    )(block_owner, tot, master, momentum, sums.reshape(S * units, half, cols),
      bases.reshape(S * SLOTS, BLOCK_ROWS, cols)))


def solution(mesh):
    return jax.shard_map(
        on_device,
        mesh=mesh,
        in_specs=(P("replica", "shard", None), P("shard", "replica"), P("shard", "replica"), P()),
        out_specs=(P("shard", "replica"), P("shard", "replica"), P(None, "replica")),
        check_vma=False,
    )
```

profile of v0, /device:TPU:0, one launch (start us, length us, event | category | flops | bytes accessed | tf_op | source)
XLA Modules:
  0.0 89.7 jit_solution(14041090652550244500)
XLA Ops:
  0.6 1.3 %copy.8.owner.owner_in = s32[8,1]{1,0:T(8,128)} copy(s32[8,1]{0,1:T(1,128)} %param.7) | data formatting | bytes 64 | tf_op args[3]
  1.9 80.1 %sync.1 = (bf16[4,20,16,1024]{3,2,1,0:T(8,128)(2,1)}, bf16[4,512,1024]{2,1,0:T(8,128)(2,1)}, f32[8,128]{1,0:T(8,128)}) custom-call(s32[8,1]{1,0:T(8,128)} %copy.8.owner.owner_in, bf16[1,512,8192]{2,1,0:T(8,128)(2,1)} %deltas.1, f32[512,1024]{1,0:T(8,128)} %master.3, f32[512,1024]{1,0:T(8,128)} %momentum.3), custom_call_target="tpu_custom_call" | custom-call | tf_op jit(solution)/shard_map/sync/pallas_call | solution.py:439
  82.0 7.7 %finish.1 = (f32[512,1024]{1,0:T(8,128)}, f32[512,1024]{1,0:T(8,128)}, bf16[1024,1024]{1,0:T(8,128)(2,1)}) custom-call(s32[8,1]{1,0:T(8,128)} %copy.8.owner.owner_in, f32[8,128]{1,0:T(8,128)} %get-tuple-element.6.tot, f32[512,1024]{1,0:T(8,128)} %master.3, f32[512,1024]{1,0:T(8,128)} %momentum.3, bf16[20,64,1024]{2,1,0:T(8,128)(2,1)} %bitcast.3, ...), custom_call_target="tpu_custom_call" | custom-call | tf_op jit(solution)/shard_map/finish/pallas_call | solution.py:477
where the time goes:
time: 90 us; the launch traced here: 89.7 us
  Pallas kernels  87.7 us (97%)
  local copies, waits for them, and re-layouts  1.32 us (1%)
    pallas_call x1, Pallas kernels, on_device(): pl.pallas_call(functools.partial(sync_kernel, R, S, rows, rc), out_shape=...  80.1 us
    pallas_call x1, Pallas kernels, on_device(): pl.pallas_call(functools.partial(finish_kernel, R, units), out_shape=(jax...  7.66 us

commit v1 on v0

--- a/solution.py
+++ b/solution.py
@@ -22,7 +22,7 @@
 
 
 def shard_count(owner, shard):
-    return sum(jnp.where(owner[b, 0] == shard, 1, 0) for b in range(owner.shape[0]))
+    return sum(jnp.where(owner[0, b] == shard, 1, 0) for b in range(owner.shape[1]))
 
 
 def spread(condition, shape):
@@ -71,8 +71,8 @@
     load_momentum = pltpu.make_async_copy(momentum, mm, lm.at[1])
     load_master.start()
     load_momentum.start()
-    mine_count = jnp.sum(jnp.where(owner[...] == me_s, 1, 0), axis=0, keepdims=True)
-    twin_count = jnp.sum(jnp.where(owner[...] == twin, 1, 0), axis=0, keepdims=True)
+    mine_count = jnp.sum(jnp.where(owner[...] == me_s, 1, 0), axis=1, keepdims=True)
+    twin_count = jnp.sum(jnp.where(owner[...] == twin, 1, 0), axis=1, keepdims=True)
     heavy = jnp.maximum(mine_count, twin_count) >= SLOTS
     pl.semaphore_wait(barrier, R + S - 2)
 
@@ -313,7 +313,7 @@
     owner, owner_s, ms, mm, su, pb, ps,
     a_s, b_s, u_s, p_s, q_s, oa_s, ob_s, op_s,
 ):
-    blocks = owner.shape[0]
+    blocks = owner.shape[1]
     cols = master.shape[1]
     half = BLOCK_ROWS // 2
     me_s = lax.axis_index("shard")
@@ -346,8 +346,8 @@
         ]
 
     def get_block(b):
-        shard = owner[b, 0]
-        place = sum(jnp.where(jnp.logical_and(owner[k, 0] == shard, k < b), 1, 0) for k in range(blocks))
+        shard = owner[0, b]
+        place = sum(jnp.where(jnp.logical_and(owner[0, k] == shard, k < b), 1, 0) for k in range(blocks))
         return [pltpu.make_async_copy(bases.at[shard * SLOTS + place], pb.at[b], p_s.at[b])] + [
             pltpu.make_async_copy(sums.at[unit(shard, place, h)], ps.at[2 * b + h], q_s.at[2 * b + h])
             for h in range(2)
@@ -419,6 +419,7 @@
     R, S = lax.axis_size("replica"), lax.axis_size("shard")
     width, cols = deltas.shape[2], master.shape[1]
     blocks = block_owner.shape[0]
+    block_owner = block_owner.reshape(1, blocks)
     half = BLOCK_ROWS // 2
     quad = S == 4 and blocks - SLOTS - (S - 2) <= 2
     rows = 2 * BLOCK_ROWS + half if quad else SLOTS * BLOCK_ROWS
@@ -484,7 +485,7 @@
         in_specs=[in_vmem, in_vmem] + [anywhere] * 4,
         out_specs=(anywhere,) * 3,
         scratch_shapes=[
-            pltpu.SMEM((blocks, 1), jnp.int32), dma,
+            pltpu.SMEM((1, blocks), jnp.int32), dma,
             vmem(master.shape, F32),
             vmem(master.shape, F32),
             vmem((2 * SLOTS, half, cols), BF16),

time: 90 us -> 88.5 us (0.983)
  local copies, waits for them, and re-layouts: 1.32 us -> 0 us
    unnamed x1 -> x0, local copies, waits for them, and re-layouts: 1.32 us -> none
where the time goes in v1:
time: 88.5 us; the launch traced here: 88.3 us
  Pallas kernels  87.7 us (99%)
    pallas_call x1, Pallas kernels, on_device(): pl.pallas_call(functools.partial(sync_kernel, R, S, rows, rc), out_shape=...  80 us
    pallas_call x1, Pallas kernels, on_device(): pl.pallas_call(functools.partial(finish_kernel, R, units), out_shape=(jax...  7.63 us

profile of v1, /device:TPU:0, one launch (start us, length us, event | category | flops | bytes accessed | tf_op | source)
XLA Modules:
  0.0 88.3 jit_solution(13012065413328563608)
XLA Ops:
  0.6 80.0 %sync.1 = (bf16[4,20,16,1024]{3,2,1,0:T(8,128)(2,1)}, bf16[4,512,1024]{2,1,0:T(8,128)(2,1)}, f32[8,128]{1,0:T(8,128)}) custom-call(s32[1,8]{1,0:T(1,128)} %bitcast.5, bf16[1,512,8192]{2,1,0:T(8,128)(2,1)} %deltas.1, f32[512,1024]{1,0:T(8,128)} %master.3, f32[512,1024]{1,0:T(8,128)} %momentum.3), custom_call_target="tpu_custom_call" | custom-call | tf_op jit(solution)/shard_map/sync/pallas_call | solution.py:440
  80.7 7.6 %finish.1 = (f32[512,1024]{1,0:T(8,128)}, f32[512,1024]{1,0:T(8,128)}, bf16[1024,1024]{1,0:T(8,128)(2,1)}) custom-call(s32[1,8]{1,0:T(1,128)} %bitcast.6, f32[8,128]{1,0:T(8,128)} %get-tuple-element.6.tot, f32[512,1024]{1,0:T(8,128)} %master.3, f32[512,1024]{1,0:T(8,128)} %momentum.3, bf16[20,64,1024]{2,1,0:T(8,128)(2,1)} %bitcast.4, ...), custom_call_target="tpu_custom_call" | custom-call | tf_op jit(solution)/shard_map/finish/pallas_call | solution.py:478

commit v2 on v1

--- a/solution.py
+++ b/solution.py
@@ -306,8 +306,420 @@
             f_copy(i, c).wait()
 
 
+def tree_kernel(
+    R, S, rows, rc, first,
+    owner, deltas, master, momentum,
+    sums, bases, tot,
+    dv, p3, yt, ms, mm, base, b3, b3_in,
+    xin, pair, zq, comb, zin, qb, combb, zinb, part_b, keep_b, xin_b, mine, norm, total_row, nbuf,
+    ld, lm, p3_s, p3_r, t_s, t_r, x_s, x_r, q_s, q_r, far_s, far_r,
+    qb_s, qb_r, farb_s, farb_r, xb_s, xb_r,
+    l_s, c_s, c_r, y_s, y_r, f_s, f_r,
+    b3_s, b3_r, bl_s, bc_s, bc_r, by_s, by_r, bf_s, bf_r, n_s, n_r,
+):
+    width = deltas.shape[2]
+    cols = width // R
+    Z = R // 2
+    per = BLOCK_ROWS // rc
+    half = BLOCK_ROWS // 2
+    chunks = rows // rc
+    whole = rows // BLOCK_ROWS
+    direct = whole * per
+    top = whole * BLOCK_ROWS
+    me_r, me_s = lax.axis_index("replica"), lax.axis_index("shard")
+    z, x = me_r // 2, me_r % 2
+    o, core = me_s // 2, me_s % 2
+    side = z // 2
+    inner = (z + side) % 2
+    outer = 1 - inner
+    is_inner, is_outer = inner == 1, inner == 0
+    x_peer = (z * 2 + 1 - x, me_s)
+    near = ((side * 2 + 1 - z % 2) * 2 + x, me_s)
+    far_outer = ((Z - 1) * (1 - side) * 2 + x, me_s)
+    far_inner = ((Z - 1 - z) * 2 + x, me_s)
+    twin = o * 2 + 1 - core
+    twin_device = (me_r, twin)
+    y_shard = (1 - o) * 2 + core
+    y_device = (me_r, y_shard)
+
+    barrier = pltpu.get_barrier_semaphore()
+    me = me_r * S + me_s
+
+    def peer(i):
+        other = (me + i) % (R * S)
+        return (other // S, other % S)
+
+    for i in range(1, R * S):
+        pl.semaphore_signal(barrier, inc=1, device_id=peer(i), device_id_type=pl.DeviceIdType.MESH)
+
+    def load(k):
+        part = pl.ds(k * BLOCK_ROWS, BLOCK_ROWS)
+        return pltpu.make_async_copy(deltas.at[0, part, :], dv.at[part, :], ld.at[k])
+
+    load(whole).start()
+    for k in range(whole):
+        load(k).start()
+    load_master = pltpu.make_async_copy(master, ms, lm.at[0])
+    load_momentum = pltpu.make_async_copy(momentum, mm, lm.at[1])
+    load_master.start()
+    load_momentum.start()
+    mine_count = jnp.sum(jnp.where(owner[...] == me_s, 1, 0), axis=1, keepdims=True)
+    twin_count = jnp.sum(jnp.where(owner[...] == twin, 1, 0), axis=1, keepdims=True)
+    heavy = jnp.maximum(mine_count, twin_count) >= SLOTS
+    norm[...] = jnp.zeros((8, 128), F32)
+    pl.semaphore_wait(barrier, R * S - 1)
+
+    def rows_of(c):
+        return pl.ds(pl.multiple_of(c * rc, rc), rc)
+
+    def columns(k, side_x):
+        e = (Z - k - outer) % Z
+        d = e + side * (Z - 1 - 2 * e)
+        return pl.ds(pl.multiple_of((d * 2 + side_x) * cols, cols), cols)
+
+    def x_copy(source, c, k):
+        return remote(
+            source.at[rows_of(c), columns(k, 1 - x)], xin.at[c, k], x_s.at[c, k], x_r.at[c, k], x_peer
+        )
+
+    def q_copy(c, k):
+        slot = 2 * inner if k == 0 else k
+        return remote(pair.at[c, k], zq.at[c, slot], q_s.at[c, k], q_r.at[c, slot], near)
+
+    def q_wait(c, slot):
+        remote(pair.at[c, slot], zq.at[c, slot], q_s.at[c, slot], q_r.at[c, slot], near).wait_recv()
+
+    def far_copy(c, i):
+        return remote(comb.at[c, i], zin.at[c], far_s.at[c, i], far_r.at[c], far_inner if i else far_outer)
+
+    def half_x(v):
+        return x if v else 1 - x
+
+    def qb_copy(c, v, k):
+        slot = 2 * inner if k == 0 else k
+        return remote(
+            deltas.at[0, rows_of(c), columns(k, half_x(v))], qb.at[c, v, slot],
+            qb_s.at[c, v, k], qb_r.at[c, v, slot], near,
+        )
+
+    def qb_wait(c, v, slot):
+        remote(
+            combb.at[c, v, 0], qb.at[c, v, slot], qb_s.at[c, v, slot], qb_r.at[c, v, slot], near
+        ).wait_recv()
+
+    def farb_copy(c, v, i):
+        return remote(
+            combb.at[c, v, i], zinb.at[c, v], farb_s.at[c, v, i], farb_r.at[c, v], far_inner if i else far_outer
+        )
+
+    def xb_copy(c):
+        return remote(part_b.at[c], xin_b.at[c], xb_s.at[c], xb_r.at[c], x_peer)
+
+    def c_copy(c):
+        return remote(mine.at[c], sums.at[me_s, c], c_s.at[c], c_r.at[c], twin_device)
+
+    def l_copy(c):
+        return pltpu.make_async_copy(mine.at[c], sums.at[me_s, c], l_s.at[c])
+
+    def y_copy(c):
+        return remote(mine.at[c], sums.at[me_s, c], y_s.at[c], y_r.at[c], y_device)
+
+    def f_copy(c):
+        return remote(sums.at[y_shard, c], sums.at[y_shard, c], f_s.at[c], f_r.at[c], twin_device)
+
+    def by_copy():
+        return remote(base, bases.at[me_s], by_s, by_r, y_device)
+
+    def bf_copy():
+        return remote(bases.at[y_shard], bases.at[y_shard], bf_s, bf_r, twin_device)
+
+    def b3_copy():
+        return remote(b3, b3_in, b3_s, b3_r, twin_device)
+
+    def base_twin():
+        return remote(base, bases.at[me_s], bc_s, bc_r, twin_device)
+
+    def base_local():
+        return pltpu.make_async_copy(base, bases.at[me_s], bl_s)
+
+    def third_copy(h):
+        return remote(
+            deltas.at[0, pl.ds((SLOTS - 1) * BLOCK_ROWS + h * half, half), :],
+            p3.at[pl.ds(h * half, half), :], p3_s.at[h], p3_r.at[h], twin_device,
+        )
+
+    def t_copy():
+        return remote(dv.at[pl.ds(top + half, half), :], yt, t_s, t_r, y_device)
+
+    def start_x(source, low, high):
+        @pl.loop(low, high)
+        def _(c):
+            for k in range(Z):
+                x_copy(source, c, k).start()
+
+    def start_qb(c):
+        for v in range(2):
+            qb_copy(c, v, 0).start()
+
+            @pl.when(is_outer)
+            def _():
+                for k in range(1, Z - 1):
+                    qb_copy(c, v, k).start()
+
+    def pick(condition, other, start, other_start):
+        @pl.loop(0, half // 16)
+        def _(r):
+            keep = spread(condition, (16, 1024))
+            for q in range(width // 1024):
+                at = (pl.ds(pl.multiple_of(start + r * 16, 16), 16), pl.ds(q * 1024, 1024))
+                there = (pl.ds(pl.multiple_of(other_start + r * 16, 16), 16), pl.ds(q * 1024, 1024))
+                dv[at] = jnp.where(keep, dv[at].astype(F32), other[there].astype(F32)).astype(BF16)
+
+    third_copy(1).start()
+    third_copy(0).start()
+    start_x(deltas.at[0], first, first + 1)
+
+    @pl.loop(0, first)
+    def _(c):
+        start_qb(c)
+
+    start_x(deltas.at[0], first + 1, direct)
+
+    def send_third():
+        load(whole).wait()
+        third_copy(1).wait_recv()
+        pick(mine_count >= SLOTS, p3, top + half, half)
+        t_copy().start()
+
+    def start_base(low, high, target, target_start):
+        @pl.loop(low * BLOCK_ROWS // 16, high * BLOCK_ROWS // 16)
+        def _(r):
+            at = pl.ds(pl.multiple_of(r * 16, 16), 16)
+            to = pl.ds(pl.multiple_of(r * 16 - target_start, 16), 16)
+            target[to, :] = (ms[at, :] - 0.567 * mm[at, :]).astype(BF16)
+
+    def make_base():
+        load_master.wait()
+        load_momentum.wait()
+        start_base(SLOTS - 1, SLOTS, b3, (SLOTS - 1) * BLOCK_ROWS)
+        b3_copy().start()
+        start_base(0, SLOTS - 1, base, 0)
+
+    def send_base():
+        b3_copy().wait_recv()
+
+        @pl.loop(0, BLOCK_ROWS // 16)
+        def _(r):
+            at = pl.ds(pl.multiple_of(top + r * 16, 16), 16)
+            there = pl.ds(pl.multiple_of(r * 16, 16), 16)
+            keep = spread(mine_count >= SLOTS, (16, cols))
+            base[at, :] = jnp.where(keep, base[at, :].astype(F32), b3_in[there, :].astype(F32)).astype(BF16)
+
+        by_copy().start()
+        base_twin().start()
+        base_local().start()
+
+    def add_pair(c):
+        @pl.when(jnp.logical_and(c % per == 0, c < direct))
+        def _():
+            load(c // per).wait()
+
+        for k in range(Z):
+            x_copy(deltas.at[0], c, k).wait_recv()
+            pair[c, k] = (xin[c, k].astype(F32) + dv[rows_of(c), columns(k, x)].astype(F32)).astype(BF16)
+            if k == 0:
+                q_copy(c, k).start()
+            elif k < Z - 1:
+                @pl.when(is_outer)
+                def _():
+                    q_copy(c, k).start()
+
+    def add_mid(c):
+        for i in range(2):
+            q_wait(c, i)
+            comb[c, i] = (pair[c, 1 + i].astype(F32) + zq[c, i].astype(F32)).astype(BF16)
+            far_copy(c, i).start()
+
+    def add_mid_b(c):
+        for v in range(2):
+            for i in range(2):
+                qb_wait(c, v, i)
+                own = dv[rows_of(c), columns(1 + i, half_x(v))].astype(F32)
+                combb[c, v, i] = (own + qb[c, v, i].astype(F32)).astype(BF16)
+                farb_copy(c, v, i).start()
+
+    def add_line_b(c):
+        for v in range(2):
+            qb_wait(c, v, 2)
+            farb_copy(c, v, 0).wait_recv()
+            own = dv[rows_of(c), columns(Z - 1, half_x(v))].astype(F32)
+            value = own + qb[c, v, 2].astype(F32) + zinb[c, v].astype(F32)
+            if v:
+                keep_b[c] = value
+            else:
+                part_b[c] = value.astype(BF16)
+                xb_copy(c).start()
+
+    def emit(c, get):
+        place = jnp.where(c >= direct, -1, c // per)
+        live = spread(place < mine_count, (8, 128))
+        part = jnp.zeros((8, 128), F32)
+        for r in range(0, rc, 16):
+            total = get(r) / R
+            mine[c, r:r + 16, :] = total.astype(BF16)
+            for h in range(0, 16, 8):
+                for q in range(0, cols, 128):
+                    v = total[h:h + 8, q:q + 128]
+                    part = part + v * v
+        norm[...] = norm[...] + jnp.where(live, part, 0.0)
+        y_copy(c).start()
+        c_copy(c).start()
+        l_copy(c).start()
+
+    def add_line(c):
+        q_wait(c, 2)
+        far_copy(c, 0).wait_recv()
+        emit(c, lambda r: (
+            pair[c, Z - 1, r:r + 16, :].astype(F32) + zq[c, 2, r:r + 16, :].astype(F32)
+            + zin[c, r:r + 16, :].astype(F32)
+        ))
+
+    def add_last_b(c):
+        xb_copy(c).wait_recv()
+        emit(c, lambda r: keep_b[c, r:r + 16, :] + xin_b[c, r:r + 16, :].astype(F32))
+
+    def forward(c):
+        y_copy(c).wait_recv()
+        f_copy(c).start()
+
+    make_base()
+    send_third()
+    send_base()
+    load(0).wait()
+
+    mid_lag, line_lag = 2, 4
+    steps = chunks - first
+    quad_at = (direct - first) * 2 // 3
+
+    @pl.loop(0, steps + line_lag)
+    def _(t):
+        @pl.when(t == direct - first)
+        def _():
+            @pl.loop(0, first)
+            def _(c):
+                add_last_b(c)
+
+        @pl.when(t < steps)
+        def _():
+            add_pair(first + t)
+
+        @pl.when(jnp.logical_and(is_inner, t < first))
+        def _():
+            add_mid_b(t)
+
+        @pl.when(jnp.logical_and(t >= 2, t < 2 + first))
+        def _():
+            add_line_b(t - 2)
+
+        @pl.when(jnp.logical_and(is_inner, jnp.logical_and(t >= mid_lag, t < steps + mid_lag)))
+        def _():
+            add_mid(first + t - mid_lag)
+
+        @pl.when(t >= line_lag)
+        def _():
+            add_line(first + t - line_lag)
+
+        @pl.when(t == quad_at)
+        def _():
+            third_copy(0).wait_recv()
+            pick(mine_count >= SLOTS, p3, top, 0)
+            t_copy().wait_recv()
+            pick(heavy, yt, top, 0)
+            start_x(dv, direct, chunks)
+
+    total_row[...] = jnp.sum(norm[...], axis=0, keepdims=True)
+
+    def n_copy(i):
+        return remote(total_row, nbuf.at[i - 1], n_s.at[i - 1], n_r.at[i - 1], peer(i))
+
+    for i in range(1, R * S):
+        n_copy(i).start()
+    by_copy().wait_recv()
+    bf_copy().start()
+
+    @pl.loop(first, chunks - 2)
+    def _(c):
+        forward(c)
+
+    @pl.loop(0, first)
+    def _(c):
+        forward(c)
+
+    @pl.loop(chunks - 2, chunks)
+    def _(c):
+        forward(c)
+
+    third_copy(0).wait_send()
+    third_copy(1).wait_send()
+    t_copy().wait_send()
+    b3_copy().wait_send()
+    base_local().wait()
+    base_twin().wait()
+
+    @pl.loop(first, chunks)
+    def _(c):
+        for k in range(Z):
+            x_copy(deltas.at[0], c, k).wait_send()
+        q_copy(c, 0).wait_send()
+
+        @pl.when(is_outer)
+        def _():
+            for k in range(1, Z - 1):
+                q_copy(c, k).wait_send()
+
+        @pl.when(is_inner)
+        def _():
+            for i in range(2):
+                far_copy(c, i).wait_send()
+
+    @pl.loop(0, first)
+    def _(c):
+        xb_copy(c).wait_send()
+        for v in range(2):
+            qb_copy(c, v, 0).wait_send()
+
+            @pl.when(is_outer)
+            def _():
+                for k in range(1, Z - 1):
+                    qb_copy(c, v, k).wait_send()
+
+            @pl.when(is_inner)
+            def _():
+                for i in range(2):
+                    farb_copy(c, v, i).wait_send()
+
+    @pl.loop(0, chunks)
+    def _(c):
+        l_copy(c).wait()
+        c_copy(c).wait()
+        y_copy(c).wait_send()
+        f_copy(c).wait()
+
+    by_copy().wait_send()
+    bf_copy().wait()
+    total = total_row[...]
+    for i in range(1, R * S):
+        n_copy(i).wait_recv()
+        total = total + nbuf[i - 1]
+    tot[...] = jnp.broadcast_to(total, (8, 128)) * jnp.where(
+        lax.broadcasted_iota(jnp.int32, (8, 128), 0) == 0, 1.0, 0.0
+    )
+    for i in range(1, R * S):
+        n_copy(i).wait_send()
+
+
 def finish_kernel(
-    R, units,
+    R, units, held,
     owner_in, tot, master, momentum, sums, bases,
     master_out, momentum_out, params,
     owner, owner_s, ms, mm, su, pb, ps,
@@ -348,7 +760,10 @@
     def get_block(b):
         shard = owner[0, b]
         place = sum(jnp.where(jnp.logical_and(owner[0, k] == shard, k < b), 1, 0) for k in range(blocks))
-        return [pltpu.make_async_copy(bases.at[shard * SLOTS + place], pb.at[b], p_s.at[b])] + [
+        kept = shard * held + place
+        if held < SLOTS:
+            kept = jnp.where(place < held, kept, (shard + 1 - 2 * (shard % 2)) * held + held - 1)
+        return [pltpu.make_async_copy(bases.at[kept], pb.at[b], p_s.at[b])] + [
             pltpu.make_async_copy(sums.at[unit(shard, place, h)], ps.at[2 * b + h], q_s.at[2 * b + h])
             for h in range(2)
         ]
@@ -436,47 +851,103 @@
     anywhere = pl.BlockSpec(memory_space=pl.ANY)
     in_vmem = pl.BlockSpec(memory_space=pltpu.VMEM)
     in_smem = pl.BlockSpec(memory_space=pltpu.SMEM)
-    ys, zs = max(O - 1, 1), max(Z - 1, 1)
-    sums, bases, tot = pl.pallas_call(
-        functools.partial(sync_kernel, R, S, rows, rc),
-        out_shape=(
-            jax.ShapeDtypeStruct((S, chunks, rc, cols), BF16),
-            jax.ShapeDtypeStruct((S,) + master.shape, BF16),
-            jax.ShapeDtypeStruct((8, 128), F32),
-        ),
-        in_specs=[in_vmem, anywhere, anywhere, anywhere],
-        out_specs=(anywhere, anywhere, in_vmem),
-        scratch_shapes=[
-            vmem((loads * BLOCK_ROWS, width), BF16),
-            vmem((BLOCK_ROWS, width) if quad else (16, 128), BF16),
-            vmem((half, width) if quad else (16, 128), BF16),
-            vmem(master.shape, F32),
-            vmem(master.shape, F32),
-            vmem(master.shape, BF16),
-            vmem((chunks, Z, rc, cols), BF16),
-            vmem((chunks, Z, rc, cols), BF16),
-            vmem((chunks, zs, rc, cols), BF16),
-            vmem((chunks, rc, cols), BF16),
-            vmem((2, 8, 128), F32),
-            vmem((R - 1, 8, 128), F32),
-            vmem((S - 1, 8, 128), F32),
-            dma((loads,)), dma((2,)), dma((2,)), dma((2,)), dma, dma,
-            dma((chunks, Z)), dma((chunks, Z)),
-            dma((chunks, zs)), dma((chunks, zs)),
-            dma((chunks,)), dma((chunks,)), dma((chunks,)),
-            dma((ys, chunks)), dma((ys, chunks)), dma((ys, chunks)), dma((ys, chunks)),
-            dma, dma, dma,
-            dma((ys,)), dma((ys,)), dma((ys,)), dma((ys,)),
-            dma((R - 1,)), dma((R - 1,)), dma((S - 1,)), dma((S - 1,)),
-        ],
-        compiler_params=pltpu.CompilerParams(
-            collective_id=0, has_side_effects=True, vmem_limit_bytes=VMEM_LIMIT
-        ),
-        name="sync",
-    )(block_owner, deltas, master, momentum)
+    tree = quad and Z == 4 and O == 2
+    held = SLOTS - 1 if tree else SLOTS
+    if tree:
+        first = chunks * 3 // 20
+        piece = (rc, cols)
+        sums, bases, tot = pl.pallas_call(
+            functools.partial(tree_kernel, R, S, rows, rc, first),
+            out_shape=(
+                jax.ShapeDtypeStruct((S, chunks, rc, cols), BF16),
+                jax.ShapeDtypeStruct((S, held * BLOCK_ROWS, cols), BF16),
+                jax.ShapeDtypeStruct((8, 128), F32),
+            ),
+            in_specs=[in_vmem, anywhere, anywhere, anywhere],
+            out_specs=(anywhere, anywhere, in_vmem),
+            scratch_shapes=[
+                vmem((loads * BLOCK_ROWS, width), BF16),
+                vmem((BLOCK_ROWS, width), BF16),
+                vmem((half, width), BF16),
+                vmem(master.shape, F32),
+                vmem(master.shape, F32),
+                vmem((held * BLOCK_ROWS, cols), BF16),
+                vmem((BLOCK_ROWS, cols), BF16),
+                vmem((BLOCK_ROWS, cols), BF16),
+                vmem((chunks, Z) + piece, BF16),
+                vmem((chunks, Z) + piece, BF16),
+                vmem((chunks, 3) + piece, BF16),
+                vmem((chunks, 2) + piece, BF16),
+                vmem((chunks,) + piece, BF16),
+                vmem((first, 2, 3) + piece, BF16),
+                vmem((first, 2, 2) + piece, BF16),
+                vmem((first, 2) + piece, BF16),
+                vmem((first,) + piece, BF16),
+                vmem((first,) + piece, F32),
+                vmem((first,) + piece, BF16),
+                vmem((chunks,) + piece, BF16),
+                vmem((8, 128), F32),
+                vmem((1, 128), F32),
+                vmem((R * S - 1, 1, 128), F32),
+                dma((loads,)), dma((2,)), dma((2,)), dma((2,)), dma, dma,
+                dma((chunks, Z)), dma((chunks, Z)),
+                dma((chunks, 3)), dma((chunks, 3)),
+                dma((chunks, 2)), dma((chunks,)),
+                dma((first, 2, 3)), dma((first, 2, 3)),
+                dma((first, 2, 2)), dma((first, 2)),
+                dma((first,)), dma((first,)),
+                dma((chunks,)), dma((chunks,)), dma((chunks,)),
+                dma((chunks,)), dma((chunks,)), dma((chunks,)), dma((chunks,)),
+                dma, dma, dma, dma, dma, dma, dma, dma, dma,
+                dma((R * S - 1,)), dma((R * S - 1,)),
+            ],
+            compiler_params=pltpu.CompilerParams(
+                collective_id=0, has_side_effects=True, vmem_limit_bytes=VMEM_LIMIT
+            ),
+            name="sync",
+        )(block_owner, deltas, master, momentum)
+    else:
+        ys, zs = max(O - 1, 1), max(Z - 1, 1)
+        sums, bases, tot = pl.pallas_call(
+            functools.partial(sync_kernel, R, S, rows, rc),
+            out_shape=(
+                jax.ShapeDtypeStruct((S, chunks, rc, cols), BF16),
+                jax.ShapeDtypeStruct((S,) + master.shape, BF16),
+                jax.ShapeDtypeStruct((8, 128), F32),
+            ),
+            in_specs=[in_vmem, anywhere, anywhere, anywhere],
+            out_specs=(anywhere, anywhere, in_vmem),
+            scratch_shapes=[
+                vmem((loads * BLOCK_ROWS, width), BF16),
+                vmem((BLOCK_ROWS, width) if quad else (16, 128), BF16),
+                vmem((half, width) if quad else (16, 128), BF16),
+                vmem(master.shape, F32),
+                vmem(master.shape, F32),
+                vmem(master.shape, BF16),
+                vmem((chunks, Z, rc, cols), BF16),
+                vmem((chunks, Z, rc, cols), BF16),
+                vmem((chunks, zs, rc, cols), BF16),
+                vmem((chunks, rc, cols), BF16),
+                vmem((2, 8, 128), F32),
+                vmem((R - 1, 8, 128), F32),
+                vmem((S - 1, 8, 128), F32),
+                dma((loads,)), dma((2,)), dma((2,)), dma((2,)), dma, dma,
+                dma((chunks, Z)), dma((chunks, Z)),
+                dma((chunks, zs)), dma((chunks, zs)),
+                dma((chunks,)), dma((chunks,)), dma((chunks,)),
+                dma((ys, chunks)), dma((ys, chunks)), dma((ys, chunks)), dma((ys, chunks)),
+                dma, dma, dma,
+                dma((ys,)), dma((ys,)), dma((ys,)), dma((ys,)),
+                dma((R - 1,)), dma((R - 1,)), dma((S - 1,)), dma((S - 1,)),
+            ],
+            compiler_params=pltpu.CompilerParams(
+                collective_id=0, has_side_effects=True, vmem_limit_bytes=VMEM_LIMIT
+            ),
+            name="sync",
+        )(block_owner, deltas, master, momentum)
 
     return tuple(pl.pallas_call(
-        functools.partial(finish_kernel, R, units),
+        functools.partial(finish_kernel, R, units, held),
         out_shape=(
             jax.ShapeDtypeStruct(master.shape, F32),
             jax.ShapeDtypeStruct(master.shape, F32),
@@ -497,7 +968,7 @@
         compiler_params=pltpu.CompilerParams(vmem_limit_bytes=VMEM_LIMIT),
         name="finish",
     )(block_owner, tot, master, momentum, sums.reshape(S * units, half, cols),
-      bases.reshape(S * SLOTS, BLOCK_ROWS, cols)))
+      bases.reshape(S * held, BLOCK_ROWS, cols)))
 
 
 def solution(mesh):

time: 88.5 us -> 84 us (0.949)
  Pallas kernels: 87.7 us -> 83.1 us
    pallas_call x2, Pallas kernels: 87.7 us -> 83.1 us  [the longest x1 75.3 us: on_device(): pl.pallas_call(functools.partial(tree_kernel, R, S, rows, rc, first), out...]
where the time goes in v2:
time: 84 us; the launch traced here: 83.7 us
  Pallas kernels  83.1 us (99%)
    pallas_call x1, Pallas kernels, on_device(): pl.pallas_call(functools.partial(tree_kernel, R, S, rows, rc, first), out...  75.3 us
    pallas_call x1, Pallas kernels, on_device(): pl.pallas_call(functools.partial(finish_kernel, R, units, held), out_shap...  7.76 us

profile of v2, /device:TPU:0, one launch (start us, length us, event | category | flops | bytes accessed | tf_op | source)
XLA Modules:
  0.0 83.7 jit_solution(2746936906897224564)
XLA Ops:
  0.6 75.3 %sync.1 = (bf16[4,20,16,1024]{3,2,1,0:T(8,128)(2,1)}, bf16[4,384,1024]{2,1,0:T(8,128)(2,1)}, f32[8,128]{1,0:T(8,128)}) custom-call(s32[1,8]{1,0:T(1,128)} %bitcast.5, bf16[1,512,8192]{2,1,0:T(8,128)(2,1)} %deltas.1, f32[512,1024]{1,0:T(8,128)} %master.3, f32[512,1024]{1,0:T(8,128)} %momentum.3), custom_call_target="tpu_custom_call" | custom-call | tf_op jit(solution)/shard_map/sync/pallas_call | solution.py:859
  76.0 7.8 %finish.1 = (f32[512,1024]{1,0:T(8,128)}, f32[512,1024]{1,0:T(8,128)}, bf16[1024,1024]{1,0:T(8,128)(2,1)}) custom-call(s32[1,8]{1,0:T(1,128)} %bitcast.6, f32[8,128]{1,0:T(8,128)} %get-tuple-element.6.tot, f32[512,1024]{1,0:T(8,128)} %master.3, f32[512,1024]{1,0:T(8,128)} %momentum.3, bf16[20,64,1024]{2,1,0:T(8,128)(2,1)} %bitcast.4, ...), custom_call_target="tpu_custom_call" | custom-call | tf_op jit(solution)/shard_map/finish/pallas_call | solution.py:949

commit v3 on v2

--- a/solution.py
+++ b/solution.py
@@ -312,7 +312,7 @@
     sums, bases, tot,
     dv, p3, yt, ms, mm, base, b3, b3_in,
     xin, pair, zq, comb, zin, qb, combb, zinb, part_b, keep_b, xin_b, mine, norm, total_row, nbuf,
-    ld, lm, p3_s, p3_r, t_s, t_r, x_s, x_r, q_s, q_r, far_s, far_r,
+    ld, lm, p3_s, p3_r, t_s, t_r, x_s, x_r, q_s, qa_r, qc_r, far_s, far_r,
     qb_s, qb_r, farb_s, farb_r, xb_s, xb_r,
     l_s, c_s, c_r, y_s, y_r, f_s, f_r,
     b3_s, b3_r, bl_s, bc_s, bc_r, by_s, by_r, bf_s, bf_r, n_s, n_r,
@@ -337,6 +337,7 @@
     near = ((side * 2 + 1 - z % 2) * 2 + x, me_s)
     far_outer = ((Z - 1) * (1 - side) * 2 + x, me_s)
     far_inner = ((Z - 1 - z) * 2 + x, me_s)
+    far = ((1 + inner * (Z - 2 - z) + outer * (1 - side)) * 2 + x, me_s)
     twin = o * 2 + 1 - core
     twin_device = (me_r, twin)
     y_shard = (1 - o) * 2 + core
@@ -349,8 +350,12 @@
         other = (me + i) % (R * S)
         return (other // S, other % S)
 
-    for i in range(1, R * S):
-        pl.semaphore_signal(barrier, inc=1, device_id=peer(i), device_id_type=pl.DeviceIdType.MESH)
+    for device in (x_peer, twin_device, y_device, near, far):
+        pl.semaphore_signal(barrier, inc=1, device_id=device, device_id_type=pl.DeviceIdType.MESH)
+
+    @pl.when(is_inner)
+    def _():
+        pl.semaphore_signal(barrier, inc=1, device_id=far_outer, device_id_type=pl.DeviceIdType.MESH)
 
     def load(k):
         part = pl.ds(k * BLOCK_ROWS, BLOCK_ROWS)
@@ -367,7 +372,7 @@
     twin_count = jnp.sum(jnp.where(owner[...] == twin, 1, 0), axis=1, keepdims=True)
     heavy = jnp.maximum(mine_count, twin_count) >= SLOTS
     norm[...] = jnp.zeros((8, 128), F32)
-    pl.semaphore_wait(barrier, R * S - 1)
+    pl.semaphore_wait(barrier, 5 + inner)
 
     def rows_of(c):
         return pl.ds(pl.multiple_of(c * rc, rc), rc)
@@ -377,55 +382,66 @@
         d = e + side * (Z - 1 - 2 * e)
         return pl.ds(pl.multiple_of((d * 2 + side_x) * cols, cols), cols)
 
+    def arrived(ref, sem):
+        remote(ref, ref, n_s, sem, twin_device).wait_recv()
+
+    def sent(ref, sem):
+        remote(ref, ref, sem, n_r, twin_device).wait_send()
+
     def x_copy(source, c, k):
-        return remote(
-            source.at[rows_of(c), columns(k, 1 - x)], xin.at[c, k], x_s.at[c, k], x_r.at[c, k], x_peer
-        )
-
-    def q_copy(c, k):
-        slot = 2 * inner if k == 0 else k
-        return remote(pair.at[c, k], zq.at[c, slot], q_s.at[c, k], q_r.at[c, slot], near)
-
-    def q_wait(c, slot):
-        remote(pair.at[c, slot], zq.at[c, slot], q_s.at[c, slot], q_r.at[c, slot], near).wait_recv()
+        return remote(source.at[rows_of(c), columns(k, 1 - x)], xin.at[c, k], x_s, x_r.at[c - first], x_peer)
+
+    def start_q(c, k):
+        if k == 0:
+            @pl.when(is_inner)
+            def _():
+                remote(pair.at[c, 0], zq.at[c, 2], q_s, qc_r.at[c - first], near).start()
+
+        @pl.when(is_outer)
+        def _():
+            remote(pair.at[c, k], zq.at[c, k], q_s, (qc_r if k == 2 else qa_r).at[c - first], near).start()
 
     def far_copy(c, i):
-        return remote(comb.at[c, i], zin.at[c], far_s.at[c, i], far_r.at[c], far_inner if i else far_outer)
+        return remote(comb.at[c, i], zin.at[c], far_s, far_r.at[c - first], far_inner if i else far_outer)
 
     def half_x(v):
         return x if v else 1 - x
 
-    def qb_copy(c, v, k):
-        slot = 2 * inner if k == 0 else k
-        return remote(
-            deltas.at[0, rows_of(c), columns(k, half_x(v))], qb.at[c, v, slot],
-            qb_s.at[c, v, k], qb_r.at[c, v, slot], near,
-        )
-
-    def qb_wait(c, v, slot):
-        remote(
-            combb.at[c, v, 0], qb.at[c, v, slot], qb_s.at[c, v, slot], qb_r.at[c, v, slot], near
-        ).wait_recv()
+    def start_qb(c):
+        def start(v, k, slot):
+            remote(
+                deltas.at[0, rows_of(c), columns(k, half_x(v))], qb.at[c, slot, v],
+                qb_s, qb_r.at[c, slot // 2], near,
+            ).start()
+
+        @pl.when(is_inner)
+        def _():
+            for v in range(2):
+                start(v, 0, 2)
+
+        @pl.when(is_outer)
+        def _():
+            for k in range(Z - 1):
+                for v in range(2):
+                    start(v, k, k)
 
     def farb_copy(c, v, i):
-        return remote(
-            combb.at[c, v, i], zinb.at[c, v], farb_s.at[c, v, i], farb_r.at[c, v], far_inner if i else far_outer
-        )
+        return remote(combb.at[c, v, i], zinb.at[c, v], farb_s, farb_r.at[c], far_inner if i else far_outer)
 
     def xb_copy(c):
-        return remote(part_b.at[c], xin_b.at[c], xb_s.at[c], xb_r.at[c], x_peer)
+        return remote(part_b.at[c], xin_b.at[c], xb_s, xb_r.at[c], x_peer)
 
     def c_copy(c):
-        return remote(mine.at[c], sums.at[me_s, c], c_s.at[c], c_r.at[c], twin_device)
+        return remote(mine.at[c], sums.at[me_s, c], c_s, c_r, twin_device)
 
     def l_copy(c):
-        return pltpu.make_async_copy(mine.at[c], sums.at[me_s, c], l_s.at[c])
+        return pltpu.make_async_copy(mine.at[c], sums.at[me_s, c], l_s)
 
     def y_copy(c):
-        return remote(mine.at[c], sums.at[me_s, c], y_s.at[c], y_r.at[c], y_device)
+        return remote(mine.at[c], sums.at[me_s, c], y_s, y_r.at[c], y_device)
 
     def f_copy(c):
-        return remote(sums.at[y_shard, c], sums.at[y_shard, c], f_s.at[c], f_r.at[c], twin_device)
+        return remote(sums.at[y_shard, c], sums.at[y_shard, c], f_s, f_r, twin_device)
 
     def by_copy():
         return remote(base, bases.at[me_s], by_s, by_r, y_device)
@@ -445,7 +461,7 @@
     def third_copy(h):
         return remote(
             deltas.at[0, pl.ds((SLOTS - 1) * BLOCK_ROWS + h * half, half), :],
-            p3.at[pl.ds(h * half, half), :], p3_s.at[h], p3_r.at[h], twin_device,
+            p3.at[pl.ds(h * half, half), :], p3_s, p3_r.at[h], twin_device,
         )
 
     def t_copy():
@@ -456,15 +472,6 @@
         def _(c):
             for k in range(Z):
                 x_copy(source, c, k).start()
-
-    def start_qb(c):
-        for v in range(2):
-            qb_copy(c, v, 0).start()
-
-            @pl.when(is_outer)
-            def _():
-                for k in range(1, Z - 1):
-                    qb_copy(c, v, k).start()
 
     def pick(condition, other, start, other_start):
         @pl.loop(0, half // 16)
@@ -524,41 +531,36 @@
         def _():
             load(c // per).wait()
 
+        arrived(xin.at[c], x_r.at[c - first])
         for k in range(Z):
-            x_copy(deltas.at[0], c, k).wait_recv()
             pair[c, k] = (xin[c, k].astype(F32) + dv[rows_of(c), columns(k, x)].astype(F32)).astype(BF16)
-            if k == 0:
-                q_copy(c, k).start()
-            elif k < Z - 1:
-                @pl.when(is_outer)
-                def _():
-                    q_copy(c, k).start()
+            if k < Z - 1:
+                start_q(c, k)
 
     def add_mid(c):
+        arrived(zq.at[c, pl.ds(0, 2)], qa_r.at[c - first])
         for i in range(2):
-            q_wait(c, i)
             comb[c, i] = (pair[c, 1 + i].astype(F32) + zq[c, i].astype(F32)).astype(BF16)
             far_copy(c, i).start()
 
     def add_mid_b(c):
+        arrived(qb.at[c, pl.ds(0, 2)], qb_r.at[c, 0])
         for v in range(2):
             for i in range(2):
-                qb_wait(c, v, i)
                 own = dv[rows_of(c), columns(1 + i, half_x(v))].astype(F32)
-                combb[c, v, i] = (own + qb[c, v, i].astype(F32)).astype(BF16)
+                combb[c, v, i] = (own + qb[c, i, v].astype(F32)).astype(BF16)
                 farb_copy(c, v, i).start()
 
     def add_line_b(c):
+        arrived(qb.at[c, 2], qb_r.at[c, 1])
+        arrived(zinb.at[c], farb_r.at[c])
         for v in range(2):
-            qb_wait(c, v, 2)
-            farb_copy(c, v, 0).wait_recv()
             own = dv[rows_of(c), columns(Z - 1, half_x(v))].astype(F32)
-            value = own + qb[c, v, 2].astype(F32) + zinb[c, v].astype(F32)
+            value = own + qb[c, 2, v].astype(F32) + zinb[c, v].astype(F32)
             if v:
                 keep_b[c] = value
             else:
                 part_b[c] = value.astype(BF16)
-                xb_copy(c).start()
 
     def emit(c, get):
         place = jnp.where(c >= direct, -1, c // per)
@@ -577,8 +579,8 @@
         l_copy(c).start()
 
     def add_line(c):
-        q_wait(c, 2)
-        far_copy(c, 0).wait_recv()
+        arrived(zq.at[c, 2], qc_r.at[c - first])
+        arrived(zin.at[c], far_r.at[c - first])
         emit(c, lambda r: (
             pair[c, Z - 1, r:r + 16, :].astype(F32) + zq[c, 2, r:r + 16, :].astype(F32)
             + zin[c, r:r + 16, :].astype(F32)
@@ -603,31 +605,31 @@
 
     @pl.loop(0, steps + line_lag)
     def _(t):
-        @pl.when(t == direct - first)
+        @pl.when(t < steps)
+        def _():
+            add_pair(first + t)
+
+        @pl.when(jnp.logical_and(is_inner, t < first))
+        def _():
+            add_mid_b(t)
+
+        @pl.when(jnp.logical_and(t >= 2, t < 2 + first))
+        def _():
+            add_line_b(t - 2)
+
+        @pl.when(jnp.logical_and(is_inner, jnp.logical_and(t >= mid_lag, t < steps + mid_lag)))
+        def _():
+            add_mid(first + t - mid_lag)
+
+        @pl.when(t >= line_lag)
+        def _():
+            add_line(first + t - line_lag)
+
+        @pl.when(t == steps)
         def _():
             @pl.loop(0, first)
             def _(c):
                 add_last_b(c)
-
-        @pl.when(t < steps)
-        def _():
-            add_pair(first + t)
-
-        @pl.when(jnp.logical_and(is_inner, t < first))
-        def _():
-            add_mid_b(t)
-
-        @pl.when(jnp.logical_and(t >= 2, t < 2 + first))
-        def _():
-            add_line_b(t - 2)
-
-        @pl.when(jnp.logical_and(is_inner, jnp.logical_and(t >= mid_lag, t < steps + mid_lag)))
-        def _():
-            add_mid(first + t - mid_lag)
-
-        @pl.when(t >= line_lag)
-        def _():
-            add_line(first + t - line_lag)
 
         @pl.when(t == quad_at)
         def _():
@@ -637,10 +639,14 @@
             pick(heavy, yt, top, 0)
             start_x(dv, direct, chunks)
 
+            @pl.loop(0, first)
+            def _(c):
+                xb_copy(c).start()
+
     total_row[...] = jnp.sum(norm[...], axis=0, keepdims=True)
 
     def n_copy(i):
-        return remote(total_row, nbuf.at[i - 1], n_s.at[i - 1], n_r.at[i - 1], peer(i))
+        return remote(total_row, nbuf.at[i - 1], n_s, n_r, peer(i))
 
     for i in range(1, R * S):
         n_copy(i).start()
@@ -659,63 +665,43 @@
     def _(c):
         forward(c)
 
-    third_copy(0).wait_send()
-    third_copy(1).wait_send()
+    sent(p3, p3_s)
     t_copy().wait_send()
     b3_copy().wait_send()
     base_local().wait()
     base_twin().wait()
-
-    @pl.loop(first, chunks)
-    def _(c):
-        for k in range(Z):
-            x_copy(deltas.at[0], c, k).wait_send()
-        q_copy(c, 0).wait_send()
-
-        @pl.when(is_outer)
-        def _():
-            for k in range(1, Z - 1):
-                q_copy(c, k).wait_send()
-
-        @pl.when(is_inner)
-        def _():
-            for i in range(2):
-                far_copy(c, i).wait_send()
-
-    @pl.loop(0, first)
-    def _(c):
-        xb_copy(c).wait_send()
-        for v in range(2):
-            qb_copy(c, v, 0).wait_send()
-
-            @pl.when(is_outer)
-            def _():
-                for k in range(1, Z - 1):
-                    qb_copy(c, v, k).wait_send()
-
-            @pl.when(is_inner)
-            def _():
-                for i in range(2):
-                    farb_copy(c, v, i).wait_send()
-
-    @pl.loop(0, chunks)
-    def _(c):
-        l_copy(c).wait()
-        c_copy(c).wait()
-        y_copy(c).wait_send()
-        f_copy(c).wait()
-
+    ours = pl.ds(first, steps)
+    sent(xin.at[ours], x_s)
+    sent(xin_b, xb_s)
+
+    @pl.when(is_outer)
+    def _():
+        sent(zq.at[ours], q_s)
+        sent(qb, qb_s)
+
+    @pl.when(is_inner)
+    def _():
+        sent(zin.at[ours], q_s)
+        sent(zinb, qb_s)
+        sent(comb.at[ours], far_s)
+        sent(combb, farb_s)
+
+    pltpu.make_async_copy(mine, sums.at[me_s], l_s).wait()
+    sent(mine, c_s)
+    sent(mine, y_s)
+    sent(mine, f_s)
+    arrived(sums.at[twin], c_r)
+    arrived(mine, f_r)
     by_copy().wait_send()
     bf_copy().wait()
+    arrived(nbuf, n_r)
+    sent(nbuf, n_s)
     total = total_row[...]
     for i in range(1, R * S):
-        n_copy(i).wait_recv()
         total = total + nbuf[i - 1]
     tot[...] = jnp.broadcast_to(total, (8, 128)) * jnp.where(
         lax.broadcasted_iota(jnp.int32, (8, 128), 0) == 0, 1.0, 0.0
     )
-    for i in range(1, R * S):
-        n_copy(i).wait_send()
 
 
 def finish_kernel(
@@ -854,7 +840,8 @@
     tree = quad and Z == 4 and O == 2
     held = SLOTS - 1 if tree else SLOTS
     if tree:
-        first = chunks * 3 // 20
+        first = chunks // 5
+        steps = chunks - first
         piece = (rc, cols)
         sums, bases, tot = pl.pallas_call(
             functools.partial(tree_kernel, R, S, rows, rc, first),
@@ -879,7 +866,7 @@
                 vmem((chunks, 3) + piece, BF16),
                 vmem((chunks, 2) + piece, BF16),
                 vmem((chunks,) + piece, BF16),
-                vmem((first, 2, 3) + piece, BF16),
+                vmem((first, 3, 2) + piece, BF16),
                 vmem((first, 2, 2) + piece, BF16),
                 vmem((first, 2) + piece, BF16),
                 vmem((first,) + piece, BF16),
@@ -889,17 +876,11 @@
                 vmem((8, 128), F32),
                 vmem((1, 128), F32),
                 vmem((R * S - 1, 1, 128), F32),
-                dma((loads,)), dma((2,)), dma((2,)), dma((2,)), dma, dma,
-                dma((chunks, Z)), dma((chunks, Z)),
-                dma((chunks, 3)), dma((chunks, 3)),
-                dma((chunks, 2)), dma((chunks,)),
-                dma((first, 2, 3)), dma((first, 2, 3)),
-                dma((first, 2, 2)), dma((first, 2)),
-                dma((first,)), dma((first,)),
-                dma((chunks,)), dma((chunks,)), dma((chunks,)),
-                dma((chunks,)), dma((chunks,)), dma((chunks,)), dma((chunks,)),
-                dma, dma, dma, dma, dma, dma, dma, dma, dma,
-                dma((R * S - 1,)), dma((R * S - 1,)),
+                dma((loads,)), dma((2,)), dma, dma((2,)), dma, dma,
+                dma, dma((steps,)), dma, dma((steps,)), dma((steps,)), dma, dma((steps,)),
+                dma, dma((first, 2)), dma, dma((first,)), dma, dma((first,)),
+                dma, dma, dma, dma, dma((chunks,)), dma, dma,
+                dma, dma, dma, dma, dma, dma, dma, dma, dma, dma, dma,
             ],
             compiler_params=pltpu.CompilerParams(
                 collective_id=0, has_side_effects=True, vmem_limit_bytes=VMEM_LIMIT

time: 84 us -> 75.8 us (0.902)
  Pallas kernels: 83.1 us -> 75.1 us
    pallas_call x1, Pallas kernels: 75.3 us -> 67.2 us  [on_device(): pl.pallas_call(functools.partial(tree_kernel, R, S, rows, rc, first), out...]
where the time goes in v3:
time: 75.8 us; the launch traced here: 75.7 us
  Pallas kernels  75.1 us (99%)
    pallas_call x1, Pallas kernels, on_device(): pl.pallas_call(functools.partial(tree_kernel, R, S, rows, rc, first), out...  67.2 us
    pallas_call x1, Pallas kernels, on_device(): pl.pallas_call(functools.partial(finish_kernel, R, units, held), out_shap...  7.92 us

profile of v3, /device:TPU:0, one launch (start us, length us, event | category | flops | bytes accessed | tf_op | source)
XLA Modules:
  0.0 75.7 jit_solution(1170471334391662656)
XLA Ops:
  0.6 67.2 %sync.1 = (bf16[4,20,16,1024]{3,2,1,0:T(8,128)(2,1)}, bf16[4,384,1024]{2,1,0:T(8,128)(2,1)}, f32[8,128]{1,0:T(8,128)}) custom-call(s32[1,8]{1,0:T(1,128)} %bitcast.5, bf16[1,512,8192]{2,1,0:T(8,128)(2,1)} %deltas.1, f32[512,1024]{1,0:T(8,128)} %master.3, f32[512,1024]{1,0:T(8,128)} %momentum.3), custom_call_target="tpu_custom_call" | custom-call | tf_op jit(solution)/shard_map/sync/pallas_call | solution.py:846
  67.8 7.9 %finish.1 = (f32[512,1024]{1,0:T(8,128)}, f32[512,1024]{1,0:T(8,128)}, bf16[1024,1024]{1,0:T(8,128)(2,1)}) custom-call(s32[1,8]{1,0:T(1,128)} %bitcast.6, f32[8,128]{1,0:T(8,128)} %get-tuple-element.6.tot, f32[512,1024]{1,0:T(8,128)} %master.3, f32[512,1024]{1,0:T(8,128)} %momentum.3, bf16[20,64,1024]{2,1,0:T(8,128)(2,1)} %bitcast.4, ...), custom_call_target="tpu_custom_call" | custom-call | tf_op jit(solution)/shard_map/finish/pallas_call | solution.py:930

commit v4 on v3

--- a/solution.py
+++ b/solution.py
@@ -12,6 +12,8 @@
 F32 = jnp.float32
 BF16 = jnp.bfloat16
 VMEM_LIMIT = 56 * 1024 * 1024
+SYNC_VMEM = 26 * 1024 * 1024
+CLOSE_VMEM = 12 * 1024 * 1024
 
 
 def remote(src, dst, send, recv, device):
@@ -308,14 +310,14 @@
 
 def tree_kernel(
     R, S, rows, rc, first,
-    owner, deltas, master, momentum,
-    sums, bases, tot,
-    dv, p3, yt, ms, mm, base, b3, b3_in,
-    xin, pair, zq, comb, zin, qb, combb, zinb, part_b, keep_b, xin_b, mine, norm, total_row, nbuf,
-    ld, lm, p3_s, p3_r, t_s, t_r, x_s, x_r, q_s, qa_r, qc_r, far_s, far_r,
+    owner_in, deltas, master, momentum,
+    sums, bases, tot, ms, mm,
+    owner, dv, p3, yt, b3, b3_in,
+    xin, pair, zq, comb, zin, qb, combb, zinb, part_b, keep_b, xin_b, norm, total_row, nbuf,
+    lo, ld, lm, p3_s, p3_r, t_s, t_r, x_s, x_r, q_s, qa_r, qc_r, far_s, far_r,
     qb_s, qb_r, farb_s, farb_r, xb_s, xb_r,
-    l_s, c_s, c_r, y_s, y_r, f_s, f_r,
-    b3_s, b3_r, bl_s, bc_s, bc_r, by_s, by_r, bf_s, bf_r, n_s, n_r,
+    c_s, c_r, y_s, y_r, f_s, f_r,
+    b3_s, b3_r, bc_s, bc_r, by_s, by_r, bf_s, bf_r, n_s, n_r,
 ):
     width = deltas.shape[2]
     cols = width // R
@@ -362,17 +364,17 @@
         return pltpu.make_async_copy(deltas.at[0, part, :], dv.at[part, :], ld.at[k])
 
     load(whole).start()
+    load_owner = pltpu.make_async_copy(owner_in, owner, lo)
+    load_owner.start()
     for k in range(whole):
         load(k).start()
     load_master = pltpu.make_async_copy(master, ms, lm.at[0])
     load_momentum = pltpu.make_async_copy(momentum, mm, lm.at[1])
     load_master.start()
     load_momentum.start()
-    mine_count = jnp.sum(jnp.where(owner[...] == me_s, 1, 0), axis=1, keepdims=True)
-    twin_count = jnp.sum(jnp.where(owner[...] == twin, 1, 0), axis=1, keepdims=True)
-    heavy = jnp.maximum(mine_count, twin_count) >= SLOTS
     norm[...] = jnp.zeros((8, 128), F32)
     pl.semaphore_wait(barrier, 5 + inner)
+    mine, base = sums.at[me_s], bases.at[me_s]
 
     def rows_of(c):
         return pl.ds(pl.multiple_of(c * rc, rc), rc)
@@ -434,9 +436,6 @@
     def c_copy(c):
         return remote(mine.at[c], sums.at[me_s, c], c_s, c_r, twin_device)
 
-    def l_copy(c):
-        return pltpu.make_async_copy(mine.at[c], sums.at[me_s, c], l_s)
-
     def y_copy(c):
         return remote(mine.at[c], sums.at[me_s, c], y_s, y_r.at[c], y_device)
 
@@ -454,9 +453,6 @@
 
     def base_twin():
         return remote(base, bases.at[me_s], bc_s, bc_r, twin_device)
-
-    def base_local():
-        return pltpu.make_async_copy(base, bases.at[me_s], bl_s)
 
     def third_copy(h):
         return remote(
@@ -524,7 +520,6 @@
 
         by_copy().start()
         base_twin().start()
-        base_local().start()
 
     def add_pair(c):
         @pl.when(jnp.logical_and(c % per == 0, c < direct))
@@ -576,7 +571,6 @@
         norm[...] = norm[...] + jnp.where(live, part, 0.0)
         y_copy(c).start()
         c_copy(c).start()
-        l_copy(c).start()
 
     def add_line(c):
         arrived(zq.at[c, 2], qc_r.at[c - first])
@@ -594,6 +588,10 @@
         y_copy(c).wait_recv()
         f_copy(c).start()
 
+    load_owner.wait()
+    mine_count = jnp.sum(jnp.where(owner[...] == me_s, 1, 0), axis=1, keepdims=True)
+    twin_count = jnp.sum(jnp.where(owner[...] == twin, 1, 0), axis=1, keepdims=True)
+    heavy = jnp.maximum(mine_count, twin_count) >= SLOTS
     make_base()
     send_third()
     send_base()
@@ -668,7 +666,6 @@
     sent(p3, p3_s)
     t_copy().wait_send()
     b3_copy().wait_send()
-    base_local().wait()
     base_twin().wait()
     ours = pl.ds(first, steps)
     sent(xin.at[ours], x_s)
@@ -686,7 +683,6 @@
         sent(comb.at[ours], far_s)
         sent(combb, farb_s)
 
-    pltpu.make_async_copy(mine, sums.at[me_s], l_s).wait()
     sent(mine, c_s)
     sent(mine, y_s)
     sent(mine, f_s)
@@ -705,7 +701,7 @@
 
 
 def finish_kernel(
-    R, units, held,
+    R, units,
     owner_in, tot, master, momentum, sums, bases,
     master_out, momentum_out, params,
     owner, owner_s, ms, mm, su, pb, ps,
@@ -746,10 +742,7 @@
     def get_block(b):
         shard = owner[0, b]
         place = sum(jnp.where(jnp.logical_and(owner[0, k] == shard, k < b), 1, 0) for k in range(blocks))
-        kept = shard * held + place
-        if held < SLOTS:
-            kept = jnp.where(place < held, kept, (shard + 1 - 2 * (shard % 2)) * held + held - 1)
-        return [pltpu.make_async_copy(bases.at[kept], pb.at[b], p_s.at[b])] + [
+        return [pltpu.make_async_copy(bases.at[shard * SLOTS + place], pb.at[b], p_s.at[b])] + [
             pltpu.make_async_copy(sums.at[unit(shard, place, h)], ps.at[2 * b + h], q_s.at[2 * b + h])
             for h in range(2)
         ]
@@ -803,6 +796,87 @@
                 at = pl.ds(pl.multiple_of(h * half + r * 16, 16), 16)
                 grad = factor * ps[2 * b + h, pl.ds(pl.multiple_of(r * 16, 16), 16), :].astype(F32)
                 pb[b, at, :] = (pb[b, at, :].astype(F32) - 1.33 * grad).astype(BF16)
+
+        put_block(b).start()
+
+    @pl.loop(0, SLOTS)
+    def _(j):
+        for copy in put_slot(j):
+            copy.wait()
+
+    @pl.loop(0, blocks)
+    def _(b):
+        put_block(b).wait()
+
+
+def close_kernel(
+    R, units, held,
+    owner_in, tot, master, momentum, sums, bases,
+    master_out, momentum_out, params,
+    owner, ms, mm, pb, owner_s, a_s, b_s, p_s,
+):
+    blocks = owner.shape[1]
+    cols = master.shape[1]
+    half = BLOCK_ROWS // 2
+    me_s = lax.axis_index("shard")
+    get_owner = pltpu.make_async_copy(owner_in, owner, owner_s)
+    get_owner.start()
+
+    def unit(shard, place, h):
+        moved = shard + jnp.where(place == SLOTS - 1, 1 - 2 * (shard % 2), 0)
+        if h:
+            moved = moved + jnp.where(moved // 2 == 0, 2, -2)
+        return jnp.where(place < 2, shard * units + 2 * place + h, moved * units + units - 1)
+
+    def slot_rows(j):
+        return pl.ds(pl.multiple_of(j * BLOCK_ROWS, BLOCK_ROWS), BLOCK_ROWS)
+
+    def put_slot(j):
+        return [
+            pltpu.make_async_copy(ms.at[slot_rows(j)], master_out.at[slot_rows(j)], a_s.at[j]),
+            pltpu.make_async_copy(mm.at[slot_rows(j)], momentum_out.at[slot_rows(j)], b_s.at[j]),
+        ]
+
+    def put_block(b):
+        return pltpu.make_async_copy(pb.at[b], params.at[slot_rows(b)], p_s.at[b])
+
+    total = jnp.sum(jnp.sum(tot[...], axis=1, keepdims=True), axis=0, keepdims=True)
+    limit = 0.5 * jnp.sqrt(jnp.full((1, 1), blocks * BLOCK_ROWS * R * cols, F32))
+    factor = jnp.minimum(1.0, limit / (jnp.sqrt(total) + 1e-06))
+    get_owner.wait()
+    count = shard_count(owner, me_s)
+
+    @pl.loop(0, SLOTS)
+    def _(j):
+        for h in range(2):
+            source = unit(me_s, j, h)
+
+            @pl.loop(0, half // 16)
+            def _(r):
+                at = pl.ds(pl.multiple_of(j * BLOCK_ROWS + h * half + r * 16, 16), 16)
+                old, before = master[at, :], momentum[at, :]
+                grad = factor * sums[source, pl.ds(pl.multiple_of(r * 16, 16), 16), :].astype(F32)
+                fresh = 0.9 * before + grad
+                live = spread(j < count, old.shape)
+                mm[at, :] = jnp.where(live, fresh, before)
+                ms[at, :] = jnp.where(live, old - 0.7 * (grad + 0.9 * fresh), old)
+
+        for copy in put_slot(j):
+            copy.start()
+
+    @pl.loop(0, blocks)
+    def _(b):
+        shard = owner[0, b]
+        place = sum(jnp.where(jnp.logical_and(owner[0, k] == shard, k < b), 1, 0) for k in range(blocks))
+        kept = jnp.where(place < held, shard * held + place, (shard + 1 - 2 * (shard % 2)) * held + held - 1)
+        for h in range(2):
+            source = unit(shard, place, h)
+
+            @pl.loop(0, half // 16)
+            def _(r):
+                at = pl.ds(pl.multiple_of(h * half + r * 16, 16), 16)
+                grad = factor * sums[source, pl.ds(pl.multiple_of(r * 16, 16), 16), :].astype(F32)
+                pb[b, at, :] = (bases[kept, at, :].astype(F32) - 1.33 * grad).astype(BF16)
 
         put_block(b).start()
 
@@ -836,29 +910,30 @@
     vmem = pltpu.VMEM
     anywhere = pl.BlockSpec(memory_space=pl.ANY)
     in_vmem = pl.BlockSpec(memory_space=pltpu.VMEM)
+    in_hbm = pl.BlockSpec(memory_space=pltpu.HBM)
     in_smem = pl.BlockSpec(memory_space=pltpu.SMEM)
     tree = quad and Z == 4 and O == 2
-    held = SLOTS - 1 if tree else SLOTS
     if tree:
+        held = SLOTS - 1
         first = chunks // 5
         steps = chunks - first
         piece = (rc, cols)
-        sums, bases, tot = pl.pallas_call(
+        sums, bases, tot, ms, mm = pl.pallas_call(
             functools.partial(tree_kernel, R, S, rows, rc, first),
             out_shape=(
                 jax.ShapeDtypeStruct((S, chunks, rc, cols), BF16),
                 jax.ShapeDtypeStruct((S, held * BLOCK_ROWS, cols), BF16),
                 jax.ShapeDtypeStruct((8, 128), F32),
+                jax.ShapeDtypeStruct(master.shape, F32),
+                jax.ShapeDtypeStruct(master.shape, F32),
             ),
-            in_specs=[in_vmem, anywhere, anywhere, anywhere],
-            out_specs=(anywhere, anywhere, in_vmem),
+            in_specs=[in_hbm] * 4,
+            out_specs=(in_vmem,) * 5,
             scratch_shapes=[
+                vmem(block_owner.shape, jnp.int32),
                 vmem((loads * BLOCK_ROWS, width), BF16),
                 vmem((BLOCK_ROWS, width), BF16),
                 vmem((half, width), BF16),
-                vmem(master.shape, F32),
-                vmem(master.shape, F32),
-                vmem((held * BLOCK_ROWS, cols), BF16),
                 vmem((BLOCK_ROWS, cols), BF16),
                 vmem((BLOCK_ROWS, cols), BF16),
                 vmem((chunks, Z) + piece, BF16),
@@ -872,63 +947,82 @@
                 vmem((first,) + piece, BF16),
                 vmem((first,) + piece, F32),
                 vmem((first,) + piece, BF16),
-                vmem((chunks,) + piece, BF16),
                 vmem((8, 128), F32),
                 vmem((1, 128), F32),
                 vmem((R * S - 1, 1, 128), F32),
-                dma((loads,)), dma((2,)), dma, dma((2,)), dma, dma,
+                dma, dma((loads,)), dma((2,)), dma, dma((2,)), dma, dma,
                 dma, dma((steps,)), dma, dma((steps,)), dma((steps,)), dma, dma((steps,)),
                 dma, dma((first, 2)), dma, dma((first,)), dma, dma((first,)),
-                dma, dma, dma, dma, dma((chunks,)), dma, dma,
-                dma, dma, dma, dma, dma, dma, dma, dma, dma, dma, dma,
+                dma, dma, dma, dma((chunks,)), dma, dma,
+                dma, dma, dma, dma, dma, dma, dma, dma, dma, dma,
             ],
             compiler_params=pltpu.CompilerParams(
-                collective_id=0, has_side_effects=True, vmem_limit_bytes=VMEM_LIMIT
+                collective_id=0, has_side_effects=True, vmem_limit_bytes=SYNC_VMEM
             ),
             name="sync",
-        )(block_owner, deltas, master, momentum)
-    else:
-        ys, zs = max(O - 1, 1), max(Z - 1, 1)
-        sums, bases, tot = pl.pallas_call(
-            functools.partial(sync_kernel, R, S, rows, rc),
+        )(*(pltpu.with_memory_space_constraint(a, pltpu.HBM) for a in (block_owner, deltas, master, momentum)))
+        return tuple(pl.pallas_call(
+            functools.partial(close_kernel, R, units, held),
             out_shape=(
-                jax.ShapeDtypeStruct((S, chunks, rc, cols), BF16),
-                jax.ShapeDtypeStruct((S,) + master.shape, BF16),
-                jax.ShapeDtypeStruct((8, 128), F32),
+                jax.ShapeDtypeStruct(master.shape, F32),
+                jax.ShapeDtypeStruct(master.shape, F32),
+                jax.ShapeDtypeStruct((blocks * BLOCK_ROWS, cols), BF16),
             ),
-            in_specs=[in_vmem, anywhere, anywhere, anywhere],
-            out_specs=(anywhere, anywhere, in_vmem),
+            in_specs=[in_vmem] * 6,
+            out_specs=(in_hbm,) * 3,
             scratch_shapes=[
-                vmem((loads * BLOCK_ROWS, width), BF16),
-                vmem((BLOCK_ROWS, width) if quad else (16, 128), BF16),
-                vmem((half, width) if quad else (16, 128), BF16),
+                pltpu.SMEM((1, blocks), jnp.int32),
                 vmem(master.shape, F32),
                 vmem(master.shape, F32),
-                vmem(master.shape, BF16),
-                vmem((chunks, Z, rc, cols), BF16),
-                vmem((chunks, Z, rc, cols), BF16),
-                vmem((chunks, zs, rc, cols), BF16),
-                vmem((chunks, rc, cols), BF16),
-                vmem((2, 8, 128), F32),
-                vmem((R - 1, 8, 128), F32),
-                vmem((S - 1, 8, 128), F32),
-                dma((loads,)), dma((2,)), dma((2,)), dma((2,)), dma, dma,
-                dma((chunks, Z)), dma((chunks, Z)),
-                dma((chunks, zs)), dma((chunks, zs)),
-                dma((chunks,)), dma((chunks,)), dma((chunks,)),
-                dma((ys, chunks)), dma((ys, chunks)), dma((ys, chunks)), dma((ys, chunks)),
-                dma, dma, dma,
-                dma((ys,)), dma((ys,)), dma((ys,)), dma((ys,)),
-                dma((R - 1,)), dma((R - 1,)), dma((S - 1,)), dma((S - 1,)),
+                vmem((blocks, BLOCK_ROWS, cols), BF16),
+                dma, dma((SLOTS,)), dma((SLOTS,)), dma((blocks,)),
             ],
-            compiler_params=pltpu.CompilerParams(
-                collective_id=0, has_side_effects=True, vmem_limit_bytes=VMEM_LIMIT
-            ),
-            name="sync",
-        )(block_owner, deltas, master, momentum)
+            compiler_params=pltpu.CompilerParams(vmem_limit_bytes=CLOSE_VMEM),
+            name="close",
+        )(block_owner, tot, ms, mm, sums.reshape(S * units, half, cols),
+          bases.reshape(S * held, BLOCK_ROWS, cols)))
+
+    ys, zs = max(O - 1, 1), max(Z - 1, 1)
+    sums, bases, tot = pl.pallas_call(
+        functools.partial(sync_kernel, R, S, rows, rc),
+        out_shape=(
+            jax.ShapeDtypeStruct((S, chunks, rc, cols), BF16),
+            jax.ShapeDtypeStruct((S,) + master.shape, BF16),
+            jax.ShapeDtypeStruct((8, 128), F32),
+        ),
+        in_specs=[in_vmem, anywhere, anywhere, anywhere],
+        out_specs=(anywhere, anywhere, in_vmem),
+        scratch_shapes=[
+            vmem((loads * BLOCK_ROWS, width), BF16),
+            vmem((BLOCK_ROWS, width) if quad else (16, 128), BF16),
+            vmem((half, width) if quad else (16, 128), BF16),
+            vmem(master.shape, F32),
+            vmem(master.shape, F32),
+            vmem(master.shape, BF16),
+            vmem((chunks, Z, rc, cols), BF16),
+            vmem((chunks, Z, rc, cols), BF16),
+            vmem((chunks, zs, rc, cols), BF16),
+            vmem((chunks, rc, cols), BF16),
+            vmem((2, 8, 128), F32),
+            vmem((R - 1, 8, 128), F32),
+            vmem((S - 1, 8, 128), F32),
+            dma((loads,)), dma((2,)), dma((2,)), dma((2,)), dma, dma,
+            dma((chunks, Z)), dma((chunks, Z)),
+            dma((chunks, zs)), dma((chunks, zs)),
+            dma((chunks,)), dma((chunks,)), dma((chunks,)),
+            dma((ys, chunks)), dma((ys, chunks)), dma((ys, chunks)), dma((ys, chunks)),
+            dma, dma, dma,
+            dma((ys,)), dma((ys,)), dma((ys,)), dma((ys,)),
+            dma((R - 1,)), dma((R - 1,)), dma((S - 1,)), dma((S - 1,)),
+        ],
+        compiler_params=pltpu.CompilerParams(
+            collective_id=0, has_side_effects=True, vmem_limit_bytes=VMEM_LIMIT
+        ),
+        name="sync",
+    )(block_owner, deltas, master, momentum)
 
     return tuple(pl.pallas_call(
-        functools.partial(finish_kernel, R, units, held),
+        functools.partial(finish_kernel, R, units),
         out_shape=(
             jax.ShapeDtypeStruct(master.shape, F32),
             jax.ShapeDtypeStruct(master.shape, F32),
@@ -949,7 +1043,7 @@
         compiler_params=pltpu.CompilerParams(vmem_limit_bytes=VMEM_LIMIT),
         name="finish",
     )(block_owner, tot, master, momentum, sums.reshape(S * units, half, cols),
-      bases.reshape(S * held, BLOCK_ROWS, cols)))
+      bases.reshape(S * SLOTS, BLOCK_ROWS, cols)))
 
 
 def solution(mesh):

time: 75.8 us -> 70.6 us (0.931)
  Pallas kernels: 75.1 us -> 69.8 us
    pallas_call x1, Pallas kernels: 7.92 us -> 3.78 us  [on_device(): pl.pallas_call(functools.partial(close_kernel, R, units, held), out_shape...]
    pallas_call x1, Pallas kernels: 67.2 us -> 66 us  [on_device(): pl.pallas_call(functools.partial(tree_kernel, R, S, rows, rc, first), out...]
where the time goes in v4:
time: 70.6 us; the launch traced here: 70.4 us
  Pallas kernels  69.8 us (99%)
    pallas_call x1, Pallas kernels, on_device(): pl.pallas_call(functools.partial(tree_kernel, R, S, rows, rc, first), out...  66 us
    pallas_call x1, Pallas kernels, on_device(): pl.pallas_call(functools.partial(close_kernel, R, units, held), out_shape...  3.78 us

profile of v4, /device:TPU:0, one launch (start us, length us, event | category | flops | bytes accessed | tf_op | source)
XLA Modules:
  0.0 70.4 jit_solution(14636359717278060225)
XLA Ops:
  0.6 0.0 copy-start
  0.6 66.0 %sync.1 = (bf16[4,20,16,1024]{3,2,1,0:T(8,128)(2,1)S(1)}, bf16[4,384,1024]{2,1,0:T(8,128)(2,1)S(1)}, f32[8,128]{1,0:T(8,128)S(1)}, f32[512,1024]{1,0:T(8,128)S(1)}, f32[512,1024]{1,0:T(8,128)S(1)}) custom-call(s32[1,8]{1,0:T(1,128)} %bitcast.5, bf16[1,512,8192]{2,1,0:T(8,128)(2,1)} %deltas.1, f32[512,1024]{1,0:T(8,128)} %master.1, f32[512,1024]{1,0:T(8,128)} %momentum.1), custom_call_target="tpu_custom_call" | custom-call | tf_op jit(solution)/shard_map/sync/pallas_call | solution.py:921
  66.6 0.0 copy-done
  66.7 3.8 %close.1 = (f32[512,1024]{1,0:T(8,128)}, f32[512,1024]{1,0:T(8,128)}, bf16[1024,1024]{1,0:T(8,128)(2,1)}) custom-call(s32[1,8]{1,0:T(1,128)S(1)} %bitcast.6, f32[8,128]{1,0:T(8,128)S(1)} %get-tuple-element.8.tot, f32[512,1024]{1,0:T(8,128)S(1)} %get-tuple-element.9.master, f32[512,1024]{1,0:T(8,128)S(1)} %get-tuple-element.10.momentum, ...), custom_call_target="tpu_custom_call" | custom-call | tf_op jit(solution)/shard_map/close/pallas_call | solution.py:964
Async XLA Ops:
  0.6 66.0 %copy-start = (s32[8,1]{0,1:T(1,128)S(1)}, s32[8,1]{0,1:T(1,128)}, u32[]{:S(2)}) copy-start(s32[8,1]{0,1:T(1,128)} %param.7) | copy-start | bytes 100

commit v5 on v4

--- a/solution.py
+++ b/solution.py
@@ -317,7 +317,7 @@
     lo, ld, lm, p3_s, p3_r, t_s, t_r, x_s, x_r, q_s, qa_r, qc_r, far_s, far_r,
     qb_s, qb_r, farb_s, farb_r, xb_s, xb_r,
     c_s, c_r, y_s, y_r, f_s, f_r,
-    b3_s, b3_r, bc_s, bc_r, by_s, by_r, bf_s, bf_r, n_s, n_r,
+    b3_s, b3_r, bc_s, bc_r, by_s, by_r, bf_s, bf_r, n_s, n_r, go,
 ):
     width = deltas.shape[2]
     cols = width // R
@@ -328,6 +328,9 @@
     whole = rows // BLOCK_ROWS
     direct = whole * per
     top = whole * BLOCK_ROWS
+    mid_lag, line_lag, late = 2, 4, 6
+    last = max(line_lag, late)
+    steps = chunks - first
     me_r, me_s = lax.axis_index("replica"), lax.axis_index("shard")
     z, x = me_r // 2, me_r % 2
     o, core = me_s // 2, me_s % 2
@@ -339,7 +342,6 @@
     near = ((side * 2 + 1 - z % 2) * 2 + x, me_s)
     far_outer = ((Z - 1) * (1 - side) * 2 + x, me_s)
     far_inner = ((Z - 1 - z) * 2 + x, me_s)
-    far = ((1 + inner * (Z - 2 - z) + outer * (1 - side)) * 2 + x, me_s)
     twin = o * 2 + 1 - core
     twin_device = (me_r, twin)
     y_shard = (1 - o) * 2 + core
@@ -352,12 +354,15 @@
         other = (me + i) % (R * S)
         return (other // S, other % S)
 
-    for device in (x_peer, twin_device, y_device, near, far):
+    def greet(device):
         pl.semaphore_signal(barrier, inc=1, device_id=device, device_id_type=pl.DeviceIdType.MESH)
+
+    for device in (x_peer, near, twin_device, y_device):
+        greet(device)
 
     @pl.when(is_inner)
     def _():
-        pl.semaphore_signal(barrier, inc=1, device_id=far_outer, device_id_type=pl.DeviceIdType.MESH)
+        greet(far_inner)
 
     def load(k):
         part = pl.ds(k * BLOCK_ROWS, BLOCK_ROWS)
@@ -366,14 +371,19 @@
     load(whole).start()
     load_owner = pltpu.make_async_copy(owner_in, owner, lo)
     load_owner.start()
-    for k in range(whole):
-        load(k).start()
     load_master = pltpu.make_async_copy(master, ms, lm.at[0])
     load_momentum = pltpu.make_async_copy(momentum, mm, lm.at[1])
     load_master.start()
     load_momentum.start()
+    for k in range(whole):
+        load(k).start()
     norm[...] = jnp.zeros((8, 128), F32)
-    pl.semaphore_wait(barrier, 5 + inner)
+    pl.semaphore_wait(barrier, 4 + inner)
+
+    @pl.when(is_inner)
+    def _():
+        pl.semaphore_signal(go, inc=1, device_id=far_inner, device_id_type=pl.DeviceIdType.MESH)
+
     mine, base = sums.at[me_s], bases.at[me_s]
 
     def rows_of(c):
@@ -391,7 +401,7 @@
         remote(ref, ref, sem, n_r, twin_device).wait_send()
 
     def x_copy(source, c, k):
-        return remote(source.at[rows_of(c), columns(k, 1 - x)], xin.at[c, k], x_s, x_r.at[c - first], x_peer)
+        return remote(source.at[rows_of(c), columns(k, 1 - x)], xin.at[c, k], x_s, x_r.at[c - first, k // 2], x_peer)
 
     def start_q(c, k):
         if k == 0:
@@ -442,8 +452,9 @@
     def f_copy(c):
         return remote(sums.at[y_shard, c], sums.at[y_shard, c], f_s, f_r, twin_device)
 
-    def by_copy():
-        return remote(base, bases.at[me_s], by_s, by_r, y_device)
+    def by_copy(i):
+        part = pl.ds(i * BLOCK_ROWS, BLOCK_ROWS * (SLOTS - 2 if i else 1))
+        return remote(base.at[part], bases.at[me_s, part], by_s.at[i], by_r.at[i], y_device)
 
     def bf_copy():
         return remote(bases.at[y_shard], bases.at[y_shard], bf_s, bf_r, twin_device)
@@ -506,7 +517,9 @@
         load_momentum.wait()
         start_base(SLOTS - 1, SLOTS, b3, (SLOTS - 1) * BLOCK_ROWS)
         b3_copy().start()
-        start_base(0, SLOTS - 1, base, 0)
+        start_base(0, 1, base, 0)
+        by_copy(0).start()
+        start_base(1, SLOTS - 1, base, 0)
 
     def send_base():
         b3_copy().wait_recv()
@@ -518,19 +531,33 @@
             keep = spread(mine_count >= SLOTS, (16, cols))
             base[at, :] = jnp.where(keep, base[at, :].astype(F32), b3_in[there, :].astype(F32)).astype(BF16)
 
-        by_copy().start()
+        by_copy(1).start()
         base_twin().start()
+
+    def ready():
+        @pl.loop(0, SLOTS * per)
+        def _(r):
+            at = pl.ds(pl.multiple_of(r * rc, rc), rc)
+            old, before = ms[at, :], mm[at, :]
+            live = spread(r // per < mine_count, old.shape)
+            ms[at, :] = jnp.where(live, old - 0.567 * before, old)
+            mm[at, :] = jnp.where(live, 0.9 * before, before)
 
     def add_pair(c):
         @pl.when(jnp.logical_and(c % per == 0, c < direct))
         def _():
             load(c // per).wait()
 
-        arrived(xin.at[c], x_r.at[c - first])
         for k in range(Z):
+            if k % 2 == 0:
+                arrived(xin.at[c, pl.ds(k, 2)], x_r.at[c - first, k // 2])
             pair[c, k] = (xin[c, k].astype(F32) + dv[rows_of(c), columns(k, x)].astype(F32)).astype(BF16)
-            if k < Z - 1:
+            if k < 2:
                 start_q(c, k)
+            elif k == 2:
+                @pl.when(c < chunks - late)
+                def _():
+                    start_q(c, k)
 
     def add_mid(c):
         arrived(zq.at[c, pl.ds(0, 2)], qa_r.at[c - first])
@@ -597,15 +624,15 @@
     send_base()
     load(0).wait()
 
-    mid_lag, line_lag = 2, 4
-    steps = chunks - first
     quad_at = (direct - first) * 2 // 3
 
-    @pl.loop(0, steps + line_lag)
+    @pl.when(is_inner)
+    def _():
+        pl.semaphore_wait(go, 1)
+
+    @pl.loop(0, steps)
     def _(t):
-        @pl.when(t < steps)
-        def _():
-            add_pair(first + t)
+        add_pair(first + t)
 
         @pl.when(jnp.logical_and(is_inner, t < first))
         def _():
@@ -615,19 +642,17 @@
         def _():
             add_line_b(t - 2)
 
-        @pl.when(jnp.logical_and(is_inner, jnp.logical_and(t >= mid_lag, t < steps + mid_lag)))
+        @pl.when(jnp.logical_and(is_inner, t >= mid_lag))
         def _():
             add_mid(first + t - mid_lag)
 
-        @pl.when(t >= line_lag)
+        @pl.when(jnp.logical_and(t >= line_lag, t - line_lag < steps - last))
         def _():
             add_line(first + t - line_lag)
 
-        @pl.when(t == steps)
-        def _():
-            @pl.loop(0, first)
-            def _(c):
-                add_last_b(c)
+        @pl.when(t == quad_at - 2)
+        def _():
+            ready()
 
         @pl.when(t == quad_at)
         def _():
@@ -641,6 +666,24 @@
             def _(c):
                 xb_copy(c).start()
 
+    @pl.loop(chunks - late, chunks)
+    def _(c):
+        start_q(c, 2)
+
+    @pl.when(is_inner)
+    def _():
+        @pl.loop(chunks - mid_lag, chunks)
+        def _(c):
+            add_mid(c)
+
+    @pl.loop(0, first)
+    def _(c):
+        add_last_b(c)
+
+    @pl.loop(chunks - last, chunks)
+    def _(c):
+        add_line(c)
+
     total_row[...] = jnp.sum(norm[...], axis=0, keepdims=True)
 
     def n_copy(i):
@@ -648,7 +691,8 @@
 
     for i in range(1, R * S):
         n_copy(i).start()
-    by_copy().wait_recv()
+    by_copy(0).wait_recv()
+    by_copy(1).wait_recv()
     bf_copy().start()
 
     @pl.loop(first, chunks - 2)
@@ -688,7 +732,8 @@
     sent(mine, f_s)
     arrived(sums.at[twin], c_r)
     arrived(mine, f_r)
-    by_copy().wait_send()
+    by_copy(0).wait_send()
+    by_copy(1).wait_send()
     bf_copy().wait()
     arrived(nbuf, n_r)
     sent(nbuf, n_s)
@@ -854,12 +899,10 @@
             @pl.loop(0, half // 16)
             def _(r):
                 at = pl.ds(pl.multiple_of(j * BLOCK_ROWS + h * half + r * 16, 16), 16)
-                old, before = master[at, :], momentum[at, :]
-                grad = factor * sums[source, pl.ds(pl.multiple_of(r * 16, 16), 16), :].astype(F32)
-                fresh = 0.9 * before + grad
-                live = spread(j < count, old.shape)
-                mm[at, :] = jnp.where(live, fresh, before)
-                ms[at, :] = jnp.where(live, old - 0.7 * (grad + 0.9 * fresh), old)
+                part = factor * sums[source, pl.ds(pl.multiple_of(r * 16, 16), 16), :].astype(F32)
+                grad = jnp.where(spread(j < count, part.shape), part, 0.0)
+                mm[at, :] = momentum[at, :] + grad
+                ms[at, :] = master[at, :] - 1.33 * grad
 
         for copy in put_slot(j):
             copy.start()
@@ -951,10 +994,11 @@
                 vmem((1, 128), F32),
                 vmem((R * S - 1, 1, 128), F32),
                 dma, dma((loads,)), dma((2,)), dma, dma((2,)), dma, dma,
-                dma, dma((steps,)), dma, dma((steps,)), dma((steps,)), dma, dma((steps,)),
+                dma, dma((steps, 2)), dma, dma((steps,)), dma((steps,)), dma, dma((steps,)),
                 dma, dma((first, 2)), dma, dma((first,)), dma, dma((first,)),
                 dma, dma, dma, dma((chunks,)), dma, dma,
-                dma, dma, dma, dma, dma, dma, dma, dma, dma, dma,
+                dma, dma, dma, dma, dma((2,)), dma((2,)), dma, dma, dma, dma,
+                pltpu.SemaphoreType.REGULAR,
             ],
             compiler_params=pltpu.CompilerParams(
                 collective_id=0, has_side_effects=True, vmem_limit_bytes=SYNC_VMEM

time: 70.6 us -> 68.2 us (0.966)
  Pallas kernels: 69.8 us -> 67.4 us
    pallas_call x1, Pallas kernels: 66 us -> 63.8 us  [on_device(): pl.pallas_call(functools.partial(tree_kernel, R, S, rows, rc, first), out...]
where the time goes in v5:
time: 68.2 us; the launch traced here: 68 us
  Pallas kernels  67.4 us (99%)
    pallas_call x1, Pallas kernels, on_device(): pl.pallas_call(functools.partial(tree_kernel, R, S, rows, rc, first), out...  63.8 us
    pallas_call x1, Pallas kernels, on_device(): pl.pallas_call(functools.partial(close_kernel, R, units, held), out_shape...  3.51 us

profile of v5, /device:TPU:0, one launch (start us, length us, event | category | flops | bytes accessed | tf_op | source)
XLA Modules:
  0.0 68.0 jit_solution(8448006149697922649)
XLA Ops:
  0.6 0.0 copy-start
  0.6 63.8 %sync.1 = (bf16[4,20,16,1024]{3,2,1,0:T(8,128)(2,1)S(1)}, bf16[4,384,1024]{2,1,0:T(8,128)(2,1)S(1)}, f32[8,128]{1,0:T(8,128)S(1)}, f32[512,1024]{1,0:T(8,128)S(1)}, f32[512,1024]{1,0:T(8,128)S(1)}) custom-call(s32[1,8]{1,0:T(1,128)} %bitcast.5, bf16[1,512,8192]{2,1,0:T(8,128)(2,1)} %deltas.1, f32[512,1024]{1,0:T(8,128)} %master.1, f32[512,1024]{1,0:T(8,128)} %momentum.1), custom_call_target="tpu_custom_call" | custom-call | tf_op jit(solution)/shard_map/sync/pallas_call | solution.py:964
  64.5 0.0 copy-done
  64.5 3.5 %close.1 = (f32[512,1024]{1,0:T(8,128)}, f32[512,1024]{1,0:T(8,128)}, bf16[1024,1024]{1,0:T(8,128)(2,1)}) custom-call(s32[1,8]{1,0:T(1,128)S(1)} %bitcast.6, f32[8,128]{1,0:T(8,128)S(1)} %get-tuple-element.8.tot, f32[512,1024]{1,0:T(8,128)S(1)} %get-tuple-element.9.master, f32[512,1024]{1,0:T(8,128)S(1)} %get-tuple-element.10.momentum, ...), custom_call_target="tpu_custom_call" | custom-call | tf_op jit(solution)/shard_map/close/pallas_call | solution.py:1008
Async XLA Ops:
  0.6 63.9 %copy-start = (s32[8,1]{0,1:T(1,128)S(1)}, s32[8,1]{0,1:T(1,128)}, u32[]{:S(2)}) copy-start(s32[8,1]{0,1:T(1,128)} %param.7) | copy-start | bytes 100

commit v6 on v5

--- a/solution.py
+++ b/solution.py
@@ -314,7 +314,7 @@
     sums, bases, tot, ms, mm,
     owner, dv, p3, yt, b3, b3_in,
     xin, pair, zq, comb, zin, qb, combb, zinb, part_b, keep_b, xin_b, norm, total_row, nbuf,
-    lo, ld, lm, p3_s, p3_r, t_s, t_r, x_s, x_r, q_s, qa_r, qc_r, far_s, far_r,
+    lo, ld, lm, p3_s, p3_r, t_s, t_r, x_s, x_r, xl_r, q_s, qa_r, qc_r, far_s, far_r,
     qb_s, qb_r, farb_s, farb_r, xb_s, xb_r,
     c_s, c_r, y_s, y_r, f_s, f_r,
     b3_s, b3_r, bc_s, bc_r, by_s, by_r, bf_s, bf_r, n_s, n_r, go,
@@ -328,9 +328,11 @@
     whole = rows // BLOCK_ROWS
     direct = whole * per
     top = whole * BLOCK_ROWS
-    mid_lag, line_lag, late = 2, 4, 6
+    mid_lag, line_lag = 2, 4
+    steps = chunks - first
+    late = chunks - direct
     last = max(line_lag, late)
-    steps = chunks - first
+    group = late
     me_r, me_s = lax.axis_index("replica"), lax.axis_index("shard")
     z, x = me_r // 2, me_r % 2
     o, core = me_s // 2, me_s % 2
@@ -368,13 +370,13 @@
         part = pl.ds(k * BLOCK_ROWS, BLOCK_ROWS)
         return pltpu.make_async_copy(deltas.at[0, part, :], dv.at[part, :], ld.at[k])
 
-    load(whole).start()
     load_owner = pltpu.make_async_copy(owner_in, owner, lo)
     load_owner.start()
     load_master = pltpu.make_async_copy(master, ms, lm.at[0])
     load_momentum = pltpu.make_async_copy(momentum, mm, lm.at[1])
     load_master.start()
     load_momentum.start()
+    load(whole).start()
     for k in range(whole):
         load(k).start()
     norm[...] = jnp.zeros((8, 128), F32)
@@ -390,7 +392,7 @@
         return pl.ds(pl.multiple_of(c * rc, rc), rc)
 
     def columns(k, side_x):
-        e = (Z - k - outer) % Z
+        e = (Z - 1 - k) if k < 2 else (outer if k == 2 else inner)
         d = e + side * (Z - 1 - 2 * e)
         return pl.ds(pl.multiple_of((d * 2 + side_x) * cols, cols), cols)
 
@@ -400,18 +402,16 @@
     def sent(ref, sem):
         remote(ref, ref, sem, n_r, twin_device).wait_send()
 
-    def x_copy(source, c, k):
-        return remote(source.at[rows_of(c), columns(k, 1 - x)], xin.at[c, k], x_s, x_r.at[c - first, k // 2], x_peer)
+    def x_copy(source, c, k, sem):
+        return remote(source.at[rows_of(c), columns(k, 1 - x)], xin.at[c, k], x_s, sem, x_peer)
 
     def start_q(c, k):
-        if k == 0:
-            @pl.when(is_inner)
+        if k == 2:
+            remote(pair.at[c, k], zq.at[c, k], q_s, qc_r.at[c - first], near).start()
+        else:
+            @pl.when(is_outer)
             def _():
-                remote(pair.at[c, 0], zq.at[c, 2], q_s, qc_r.at[c - first], near).start()
-
-        @pl.when(is_outer)
-        def _():
-            remote(pair.at[c, k], zq.at[c, k], q_s, (qc_r if k == 2 else qa_r).at[c - first], near).start()
+                remote(pair.at[c, k], zq.at[c, k], q_s, qa_r.at[c - first], near).start()
 
     def far_copy(c, i):
         return remote(comb.at[c, i], zin.at[c], far_s, far_r.at[c - first], far_inner if i else far_outer)
@@ -420,22 +420,19 @@
         return x if v else 1 - x
 
     def start_qb(c):
-        def start(v, k, slot):
+        def start(v, k):
             remote(
-                deltas.at[0, rows_of(c), columns(k, half_x(v))], qb.at[c, slot, v],
-                qb_s, qb_r.at[c, slot // 2], near,
+                deltas.at[0, rows_of(c), columns(k, half_x(v))], qb.at[c, k, v], qb_s, qb_r.at[c, k // 2], near
             ).start()
 
-        @pl.when(is_inner)
-        def _():
-            for v in range(2):
-                start(v, 0, 2)
-
         @pl.when(is_outer)
         def _():
-            for k in range(Z - 1):
+            for k in range(2):
                 for v in range(2):
-                    start(v, k, k)
+                    start(v, k)
+
+        for v in range(2):
+            start(v, 2)
 
     def farb_copy(c, v, i):
         return remote(combb.at[c, v, i], zinb.at[c, v], farb_s, farb_r.at[c], far_inner if i else far_outer)
@@ -447,10 +444,11 @@
         return remote(mine.at[c], sums.at[me_s, c], c_s, c_r, twin_device)
 
     def y_copy(c):
-        return remote(mine.at[c], sums.at[me_s, c], y_s, y_r.at[c], y_device)
-
-    def f_copy(c):
-        return remote(sums.at[y_shard, c], sums.at[y_shard, c], f_s, f_r, twin_device)
+        return remote(mine.at[c], sums.at[me_s, c], y_s, y_r.at[c // group], y_device)
+
+    def f_copy(g):
+        part = sums.at[y_shard, pl.ds(g * group, group)]
+        return remote(part, part, f_s, f_r, twin_device)
 
     def by_copy(i):
         part = pl.ds(i * BLOCK_ROWS, BLOCK_ROWS * (SLOTS - 2 if i else 1))
@@ -474,11 +472,17 @@
     def t_copy():
         return remote(dv.at[pl.ds(top + half, half), :], yt, t_s, t_r, y_device)
 
-    def start_x(source, low, high):
+    def start_x(low, high):
         @pl.loop(low, high)
         def _(c):
             for k in range(Z):
-                x_copy(source, c, k).start()
+                x_copy(deltas.at[0], c, k, x_r.at[c - first]).start()
+
+    def start_late(pieces):
+        @pl.loop(direct, chunks)
+        def _(c):
+            for k in pieces:
+                x_copy(dv, c, k, x_r.at[c - first] if k < 2 else xl_r.at[c - direct, k - 2]).start()
 
     def pick(condition, other, start, other_start):
         @pl.loop(0, half // 16)
@@ -490,14 +494,9 @@
                 dv[at] = jnp.where(keep, dv[at].astype(F32), other[there].astype(F32)).astype(BF16)
 
     third_copy(1).start()
+    start_x(first, first + 2)
     third_copy(0).start()
-    start_x(deltas.at[0], first, first + 1)
-
-    @pl.loop(0, first)
-    def _(c):
-        start_qb(c)
-
-    start_x(deltas.at[0], first + 1, direct)
+    start_qb(0)
 
     def send_third():
         load(whole).wait()
@@ -513,12 +512,8 @@
             target[to, :] = (ms[at, :] - 0.567 * mm[at, :]).astype(BF16)
 
     def make_base():
-        load_master.wait()
-        load_momentum.wait()
         start_base(SLOTS - 1, SLOTS, b3, (SLOTS - 1) * BLOCK_ROWS)
         b3_copy().start()
-        start_base(0, 1, base, 0)
-        by_copy(0).start()
         start_base(1, SLOTS - 1, base, 0)
 
     def send_base():
@@ -543,33 +538,23 @@
             ms[at, :] = jnp.where(live, old - 0.567 * before, old)
             mm[at, :] = jnp.where(live, 0.9 * before, before)
 
-    def add_pair(c):
-        @pl.when(jnp.logical_and(c % per == 0, c < direct))
-        def _():
-            load(c // per).wait()
-
-        for k in range(Z):
-            if k % 2 == 0:
-                arrived(xin.at[c, pl.ds(k, 2)], x_r.at[c - first, k // 2])
+    def add_pair(c, pieces):
+        for k in pieces:
             pair[c, k] = (xin[c, k].astype(F32) + dv[rows_of(c), columns(k, x)].astype(F32)).astype(BF16)
-            if k < 2:
+            if k < Z - 1:
                 start_q(c, k)
-            elif k == 2:
-                @pl.when(c < chunks - late)
-                def _():
-                    start_q(c, k)
 
     def add_mid(c):
         arrived(zq.at[c, pl.ds(0, 2)], qa_r.at[c - first])
         for i in range(2):
-            comb[c, i] = (pair[c, 1 + i].astype(F32) + zq[c, i].astype(F32)).astype(BF16)
+            comb[c, i] = (pair[c, i].astype(F32) + zq[c, i].astype(F32)).astype(BF16)
             far_copy(c, i).start()
 
     def add_mid_b(c):
         arrived(qb.at[c, pl.ds(0, 2)], qb_r.at[c, 0])
         for v in range(2):
             for i in range(2):
-                own = dv[rows_of(c), columns(1 + i, half_x(v))].astype(F32)
+                own = dv[rows_of(c), columns(i, half_x(v))].astype(F32)
                 combb[c, v, i] = (own + qb[c, i, v].astype(F32)).astype(BF16)
                 farb_copy(c, v, i).start()
 
@@ -611,14 +596,24 @@
         xb_copy(c).wait_recv()
         emit(c, lambda r: keep_b[c, r:r + 16, :] + xin_b[c, r:r + 16, :].astype(F32))
 
-    def forward(c):
-        y_copy(c).wait_recv()
-        f_copy(c).start()
+    def forward(g):
+        arrived(sums.at[y_shard, pl.ds(g * group, group)], y_r.at[g])
+        f_copy(g).start()
 
     load_owner.wait()
     mine_count = jnp.sum(jnp.where(owner[...] == me_s, 1, 0), axis=1, keepdims=True)
     twin_count = jnp.sum(jnp.where(owner[...] == twin, 1, 0), axis=1, keepdims=True)
     heavy = jnp.maximum(mine_count, twin_count) >= SLOTS
+    load_master.wait()
+    load_momentum.wait()
+    start_base(0, 1, base, 0)
+    by_copy(0).start()
+
+    @pl.loop(1, first)
+    def _(c):
+        start_qb(c)
+
+    start_x(first + 2, direct)
     make_base()
     send_third()
     send_base()
@@ -632,7 +627,21 @@
 
     @pl.loop(0, steps)
     def _(t):
-        add_pair(first + t)
+        c = first + t
+
+        @pl.when(jnp.logical_and(c % per == 0, c < direct))
+        def _():
+            load(c // per).wait()
+
+        @pl.when(c < direct)
+        def _():
+            arrived(xin.at[c], x_r.at[c - first])
+            add_pair(c, range(Z))
+
+        @pl.when(c >= direct)
+        def _():
+            arrived(xin.at[c, pl.ds(0, 2)], x_r.at[c - first])
+            add_pair(c, range(2))
 
         @pl.when(jnp.logical_and(is_inner, t < first))
         def _():
@@ -660,15 +669,17 @@
             pick(mine_count >= SLOTS, p3, top, 0)
             t_copy().wait_recv()
             pick(heavy, yt, top, 0)
-            start_x(dv, direct, chunks)
+            for pieces in ((0, 1), (2,), (3,)):
+                start_late(pieces)
 
             @pl.loop(0, first)
             def _(c):
                 xb_copy(c).start()
 
-    @pl.loop(chunks - late, chunks)
+    @pl.loop(direct, chunks)
     def _(c):
-        start_q(c, 2)
+        arrived(xin.at[c, 2], xl_r.at[c - direct, 0])
+        add_pair(c, (2,))
 
     @pl.when(is_inner)
     def _():
@@ -676,6 +687,11 @@
         def _(c):
             add_mid(c)
 
+    @pl.loop(direct, chunks)
+    def _(c):
+        arrived(xin.at[c, 3], xl_r.at[c - direct, 1])
+        add_pair(c, (3,))
+
     @pl.loop(0, first)
     def _(c):
         add_last_b(c)
@@ -695,17 +711,11 @@
     by_copy(1).wait_recv()
     bf_copy().start()
 
-    @pl.loop(first, chunks - 2)
-    def _(c):
-        forward(c)
-
-    @pl.loop(0, first)
-    def _(c):
-        forward(c)
-
-    @pl.loop(chunks - 2, chunks)
-    def _(c):
-        forward(c)
+    @pl.loop(1, chunks // group)
+    def _(g):
+        forward(g % (chunks // group - 1))
+
+    forward(chunks // group - 1)
 
     sent(p3, p3_s)
     t_copy().wait_send()
@@ -888,8 +898,7 @@
     total = jnp.sum(jnp.sum(tot[...], axis=1, keepdims=True), axis=0, keepdims=True)
     limit = 0.5 * jnp.sqrt(jnp.full((1, 1), blocks * BLOCK_ROWS * R * cols, F32))
     factor = jnp.minimum(1.0, limit / (jnp.sqrt(total) + 1e-06))
-    get_owner.wait()
-    count = shard_count(owner, me_s)
+    count = jnp.sum(jnp.where(owner_in[...] == me_s, 1, 0), axis=1, keepdims=True)
 
     @pl.loop(0, SLOTS)
     def _(j):
@@ -906,6 +915,8 @@
 
         for copy in put_slot(j):
             copy.start()
+
+    get_owner.wait()
 
     @pl.loop(0, blocks)
     def _(b):
@@ -958,7 +969,7 @@
     tree = quad and Z == 4 and O == 2
     if tree:
         held = SLOTS - 1
-        first = chunks // 5
+        first = chunks * 3 // 20
         steps = chunks - first
         piece = (rc, cols)
         sums, bases, tot, ms, mm = pl.pallas_call(
@@ -994,9 +1005,9 @@
                 vmem((1, 128), F32),
                 vmem((R * S - 1, 1, 128), F32),
                 dma, dma((loads,)), dma((2,)), dma, dma((2,)), dma, dma,
-                dma, dma((steps, 2)), dma, dma((steps,)), dma((steps,)), dma, dma((steps,)),
+                dma, dma((steps,)), dma((half // rc, 2)), dma, dma((steps,)), dma((steps,)), dma, dma((steps,)),
                 dma, dma((first, 2)), dma, dma((first,)), dma, dma((first,)),
-                dma, dma, dma, dma((chunks,)), dma, dma,
+                dma, dma, dma, dma((chunks * rc // half,)), dma, dma,
                 dma, dma, dma, dma, dma((2,)), dma((2,)), dma, dma, dma, dma,
                 pltpu.SemaphoreType.REGULAR,
             ],

time: 68.2 us -> 67 us (0.982)
  Pallas kernels: 67.4 us -> 66.2 us
    pallas_call x1, Pallas kernels: 63.8 us -> 63.1 us  [on_device(): pl.pallas_call(functools.partial(tree_kernel, R, S, rows, rc, first), out...]
where the time goes in v6:
time: 67 us; the launch traced here: 66.8 us
  Pallas kernels  66.2 us (99%)
    pallas_call x1, Pallas kernels, on_device(): pl.pallas_call(functools.partial(tree_kernel, R, S, rows, rc, first), out...  63.1 us
    pallas_call x1, Pallas kernels, on_device(): pl.pallas_call(functools.partial(close_kernel, R, units, held), out_shape...  3.05 us

profile of v6, /device:TPU:0, one launch (start us, length us, event | category | flops | bytes accessed | tf_op | source)
XLA Modules:
  0.0 66.8 jit_solution(2714326515250275958)
XLA Ops:
  0.6 0.0 copy-start
  0.6 63.1 %sync.1 = (bf16[4,20,16,1024]{3,2,1,0:T(8,128)(2,1)S(1)}, bf16[4,384,1024]{2,1,0:T(8,128)(2,1)S(1)}, f32[8,128]{1,0:T(8,128)S(1)}, f32[512,1024]{1,0:T(8,128)S(1)}, f32[512,1024]{1,0:T(8,128)S(1)}) custom-call(s32[1,8]{1,0:T(1,128)} %bitcast.5, bf16[1,512,8192]{2,1,0:T(8,128)(2,1)} %deltas.1, f32[512,1024]{1,0:T(8,128)} %master.1, f32[512,1024]{1,0:T(8,128)} %momentum.1), custom_call_target="tpu_custom_call" | custom-call | tf_op jit(solution)/shard_map/sync/pallas_call | solution.py:975
  63.8 0.0 copy-done
  63.8 3.1 %close.1 = (f32[512,1024]{1,0:T(8,128)}, f32[512,1024]{1,0:T(8,128)}, bf16[1024,1024]{1,0:T(8,128)(2,1)}) custom-call(s32[1,8]{1,0:T(1,128)S(1)} %bitcast.6, f32[8,128]{1,0:T(8,128)S(1)} %get-tuple-element.8.tot, f32[512,1024]{1,0:T(8,128)S(1)} %get-tuple-element.9.master, f32[512,1024]{1,0:T(8,128)S(1)} %get-tuple-element.10.momentum, ...), custom_call_target="tpu_custom_call" | custom-call | tf_op jit(solution)/shard_map/close/pallas_call | solution.py:1019
Async XLA Ops:
  0.6 63.1 %copy-start = (s32[8,1]{0,1:T(1,128)S(1)}, s32[8,1]{0,1:T(1,128)}, u32[]{:S(2)}) copy-start(s32[8,1]{0,1:T(1,128)} %param.7) | copy-start | bytes 100

commit v7 on v6

--- a/solution.py
+++ b/solution.py
@@ -619,7 +619,7 @@
     send_base()
     load(0).wait()
 
-    quad_at = (direct - first) * 2 // 3
+    quad_at = (direct - first) * 5 // 7
 
     @pl.when(is_inner)
     def _():
@@ -692,13 +692,15 @@
         arrived(xin.at[c, 3], xl_r.at[c - direct, 1])
         add_pair(c, (3,))
 
+    @pl.loop(chunks - last, chunks - 1)
+    def _(c):
+        add_line(c)
+
     @pl.loop(0, first)
     def _(c):
         add_last_b(c)
 
-    @pl.loop(chunks - last, chunks)
-    def _(c):
-        add_line(c)
+    add_line(chunks - 1)
 
     total_row[...] = jnp.sum(norm[...], axis=0, keepdims=True)
 
@@ -905,7 +907,7 @@
         for h in range(2):
             source = unit(me_s, j, h)
 
-            @pl.loop(0, half // 16)
+            @pl.loop(0, half // 16, unroll=4)
             def _(r):
                 at = pl.ds(pl.multiple_of(j * BLOCK_ROWS + h * half + r * 16, 16), 16)
                 part = factor * sums[source, pl.ds(pl.multiple_of(r * 16, 16), 16), :].astype(F32)
@@ -926,7 +928,7 @@
         for h in range(2):
             source = unit(shard, place, h)
 
-            @pl.loop(0, half // 16)
+            @pl.loop(0, half // 16, unroll=4)
             def _(r):
                 at = pl.ds(pl.multiple_of(h * half + r * 16, 16), 16)
                 grad = factor * sums[source, pl.ds(pl.multiple_of(r * 16, 16), 16), :].astype(F32)

time: 67 us -> 66.9 us (level)
  no operation moved by 1% of the time
where the time goes in v7:
time: 66.9 us; the launch traced here: 66.8 us
  Pallas kernels  66.1 us (99%)
    pallas_call x1, Pallas kernels, on_device(): pl.pallas_call(functools.partial(tree_kernel, R, S, rows, rc, first), out...  63.1 us
    pallas_call x1, Pallas kernels, on_device(): pl.pallas_call(functools.partial(close_kernel, R, units, held), out_shape...  3.02 us

profile of v7, /device:TPU:0, one launch (start us, length us, event | category | flops | bytes accessed | tf_op | source)
XLA Modules:
  0.0 66.8 jit_solution(1939417526318797948)
XLA Ops:
  0.6 0.0 copy-start
  0.6 63.1 %sync.1 = (bf16[4,20,16,1024]{3,2,1,0:T(8,128)(2,1)S(1)}, bf16[4,384,1024]{2,1,0:T(8,128)(2,1)S(1)}, f32[8,128]{1,0:T(8,128)S(1)}, f32[512,1024]{1,0:T(8,128)S(1)}, f32[512,1024]{1,0:T(8,128)S(1)}) custom-call(s32[1,8]{1,0:T(1,128)} %bitcast.5, bf16[1,512,8192]{2,1,0:T(8,128)(2,1)} %deltas.1, f32[512,1024]{1,0:T(8,128)} %master.1, f32[512,1024]{1,0:T(8,128)} %momentum.1), custom_call_target="tpu_custom_call" | custom-call | tf_op jit(solution)/shard_map/sync/pallas_call | solution.py:977
  63.8 0.0 copy-done
  63.8 3.0 %close.1 = (f32[512,1024]{1,0:T(8,128)}, f32[512,1024]{1,0:T(8,128)}, bf16[1024,1024]{1,0:T(8,128)(2,1)}) custom-call(s32[1,8]{1,0:T(1,128)S(1)} %bitcast.6, f32[8,128]{1,0:T(8,128)S(1)} %get-tuple-element.8.tot, f32[512,1024]{1,0:T(8,128)S(1)} %get-tuple-element.9.master, f32[512,1024]{1,0:T(8,128)S(1)} %get-tuple-element.10.momentum, ...), custom_call_target="tpu_custom_call" | custom-call | tf_op jit(solution)/shard_map/close/pallas_call | solution.py:1021
Async XLA Ops:
  0.6 63.1 %copy-start = (s32[8,1]{0,1:T(1,128)S(1)}, s32[8,1]{0,1:T(1,128)}, u32[]{:S(2)}) copy-start(s32[8,1]{0,1:T(1,128)} %param.7) | copy-start | bytes 100
